TPU v7x, 512 devices: a whole 4x8x8 slice. The times are simulated.
512 devices in a mesh: slab: 128 (over y, z, core), sub: 4 (over x).
Axes of the slice: x: 4, y: 8, z: 8, core: 2. Of those that a mesh axis runs over, the one named last changes fastest.
Arguments:
- orbitals: bfloat16 [512, 16, 110592], P(('slab', 'sub')), may hold values from -0.25 to 0.25
- occupations: int32 [512, 16], P(('slab', 'sub')), may hold values from 0 to 2, as said below
- patch_sign: int32 [512], P(('slab', 'sub')), may hold values from -1 to 1, as said below
- corners: int32 [512, 3], replicated, may hold values from 0 to 511, as said below
- core_span: int32 [512, 6], P(('slab', 'sub')), may hold values from 8 to 32, as said below
- outer_density: float32 [512, 256, 256], P('slab', 'sub'), may hold values from 0 to 0.3, as said below
Outputs:
- box_potential: float32 [512, 110592], P(('slab', 'sub'))
- potential: float32 [512, 256, 256], P('slab', 'sub')
Inputs may be any that keep to these rules, and one draw needn't show every extreme that they name: Each fragment's occupations sum to 16. patch_sign[f] is -1 raised to the number of dimensions along which fragment f's core is 16 cells long. corners[f, 0] lies in [4 * (f // 4), that + 4), the planes of the slab index that holds fragment f; corners[f, 1] lies in [0, 256) and corners[f, 2] in [0, 256). `core_span`: each core lies inside its box and is 16 or 32 cells long along each dimension; fragments 8 j to 8 j + 7 are the eight kinds of core that start at one common grid cell, a corner of the fragment division; along the second and third dimensions these corners lie at different points of one lattice of spacing 16. `outer_density`: nonnegative; zero exactly on the cells where the fragments given here have signed coverage one.
All inputs are finite; a program needn't handle non-finite values.
Results may differ from a plain program's by a relative error of at most 0.0003.
Values sent between devices are 32-bit elements; how exact they have to be, the bound alone decides.
A program may use at most 64 MiB of HBM per device.

v0:
```python
import math

import jax
import jax.numpy as jnp
from jax import lax
from jax.sharding import PartitionSpec as P

BOX = 48
NX = 256
NY = 256
Z_DEV = 4


spacing = 0.35
floor_density = 0.001


def passed_along(shard, axis, by):
    length = lax.axis_size(axis)
    return lax.ppermute(shard, axis, [(i, (i + by) % length) for i in range(length)])


def in_blocks(shard, dim, length):
    lengths = shard.shape
    blocks = shard.reshape(*lengths[:dim], length, lengths[dim] // length, *lengths[dim + 1 :])
    return jnp.moveaxis(blocks, dim, 0)


def sent_and_summed(shard, axis, dim):
    length = lax.axis_size(axis)
    blocks = lax.all_to_all(in_blocks(shard, dim, length), axis, 0, 0, tiled=True)
    return jnp.sum(blocks, axis=0)


def side_by_side(arrays, axis, split_dim, concat_dim, along):
    widths = [a.shape[along] for a in arrays]
    both = jnp.concatenate(arrays, axis=along)
    filled = lax.all_to_all(both, axis, split_axis=split_dim, concat_axis=concat_dim, tiled=True)
    return tuple(jnp.split(filled, [sum(widths[:k]) for k in range(1, len(widths))], axis=along))


def from_everyone(shard, axis):
    copies = jnp.broadcast_to(shard, (lax.axis_size(axis), *shard.shape))
    return lax.all_to_all(copies, axis, split_axis=0, concat_axis=0, tiled=True)


def laid_out(blocks, dim):
    blocks = jnp.moveaxis(blocks, 0, dim)
    lengths = blocks.shape
    return blocks.reshape(*lengths[:dim], lengths[dim] * lengths[dim + 1], *lengths[dim + 2 :])


def gathered_copies(shard, axis, dim):
    blocks = from_everyone(shard, axis)
    return laid_out(blocks, dim)


def wave_squares(index, count):
    folded = jnp.where(index > count // 2, index - count, index)
    wave = 2.0 * math.pi / (count * spacing) * folded.astype(jnp.float32)
    return wave * wave


def hartree_kernel(index_z, count_z, index_x, count_x, index_y, count_y):
    square = (
        wave_squares(index_z, count_z)[:, None, None]
        + wave_squares(index_x, count_x)[None, :, None]
        + wave_squares(index_y, count_y)[None, None, :]
    )
    safe_square = jnp.where(square > 0, square, 1.0)
    kernel = jnp.where(square > 0, 4.0 * math.pi / safe_square, 0.0)
    return kernel / float(count_z * count_x * count_y)


def exchange_correlation(density):
    clipped = jnp.maximum(density, floor_density)
    radius = jnp.cbrt(3.0 / (4.0 * math.pi * clipped))
    exchange = -jnp.cbrt(3.0 * clipped / math.pi)
    correlation = -0.44 / (radius + 7.8) - 0.44 * radius / (3.0 * (radius + 7.8) ** 2)
    return exchange + correlation


def angle_tables(count):
    index = jnp.arange(count, dtype=jnp.int32)
    product = index[:, None] * index[None, :] % count
    angle = 2.0 * math.pi / count * product.astype(jnp.float32)
    return (jnp.cos(angle), jnp.sin(angle))


def apply_axis(values, table, axis):
    if axis == 0:
        return jnp.einsum("kj,jab->kab", table, values, precision=lax.Precision.HIGHEST)
    if axis == 1:
        return jnp.einsum("kj,ajb->akb", table, values, precision=lax.Precision.HIGHEST)
    return jnp.einsum("abj,jk->abk", values, table, precision=lax.Precision.HIGHEST)


def transform(real_part, imag_part, axis, inverse):
    cosine_table, sine_table = angle_tables(real_part.shape[axis])
    cos_real = apply_axis(real_part, cosine_table, axis)
    cos_imag = apply_axis(imag_part, cosine_table, axis)
    sin_real = apply_axis(real_part, sine_table, axis)
    sin_imag = apply_axis(imag_part, sine_table, axis)
    if inverse:
        return (cos_real - sin_imag, cos_imag + sin_real)
    return (cos_real + sin_imag, cos_imag - sin_real)


def body(orbitals, occupations, patch_sign, corners, core_span, outer_density):
    slab_count = lax.axis_size("slab")
    sub_count = lax.axis_size("sub")
    slab_id = lax.axis_index("slab")
    sub_id = lax.axis_index("sub")
    reach = (BOX + Z_DEV - 2) // Z_DEV + 1
    orbital_values = orbitals[0]
    weights = occupations[0].astype(jnp.float32) * patch_sign[0].astype(jnp.float32)
    density_box = jnp.sum(weights[:, None] * jnp.square(orbital_values.astype(jnp.float32)), axis=0)
    span = core_span[0]
    cell = jnp.arange(BOX, dtype=jnp.int32)
    inside_z = (cell >= span[0]) & (cell < span[0] + span[3])
    inside_x = (cell >= span[1]) & (cell < span[1] + span[4])
    inside_y = (cell >= span[2]) & (cell < span[2] + span[5])
    inside = (inside_z[:, None, None] & inside_x[None, :, None] & inside_y[None, None, :]).reshape(
        BOX * BOX * BOX
    )
    density_box = density_box * inside.astype(jnp.float32)
    own_fragment = slab_id * sub_count + sub_id
    plane_offset = corners[own_fragment, 0] - slab_id * Z_DEV
    padded = lax.dynamic_update_slice(
        jnp.zeros((reach * Z_DEV, BOX * BOX), jnp.float32),
        density_box.reshape(BOX, BOX * BOX),
        (plane_offset, 0),
    )
    pieces = padded.reshape(reach, Z_DEV, BOX * BOX)
    moved = [pieces[distance] for distance in range(reach)]
    for level in range((reach - 1).bit_length()):
        chosen = [distance for distance in range(reach) if distance >> level & 1]
        shipped = passed_along(
            jnp.stack([moved[distance] for distance in chosen]), "slab", 1 << level
        )
        for position, distance in enumerate(chosen):
            moved[distance] = shipped[position]
    arrived = jnp.stack(moved)

    def place_piece(distance, frame):
        source = (slab_id - distance) % slab_count * sub_count + sub_id
        start_x = corners[source, 1]
        start_y = corners[source, 2]
        piece = lax.dynamic_index_in_dim(arrived, distance, 0, False).reshape(Z_DEV, BOX, BOX)
        current = lax.dynamic_slice(frame, (0, start_x, start_y), (Z_DEV, BOX, BOX))
        return lax.dynamic_update_slice(frame, current + piece, (0, start_x, start_y))

    frame = lax.fori_loop(
        0, reach, place_piece, jnp.zeros((Z_DEV, NX + BOX, NY + BOX), jnp.float32)
    )
    folded = frame[:, :NX, :NY]
    folded = folded + jnp.pad(frame[:, NX:, :NY], ((0, 0), (0, NX - BOX), (0, 0)))
    folded = folded + jnp.pad(frame[:, :NX, NY:], ((0, 0), (0, 0), (0, NY - BOX)))
    folded = folded + jnp.pad(frame[:, NX:, NY:], ((0, 0), (0, NX - BOX), (0, NY - BOX)))
    density = sent_and_summed(folded, "sub", 1) + outer_density
    cosine_table, sine_table = angle_tables(NY)
    spec_real = apply_axis(density, cosine_table, 2)
    spec_imag = -apply_axis(density, sine_table, 2)
    spec_real, spec_imag = side_by_side((spec_real, spec_imag), "sub", 2, 1, 0)
    spec_real, spec_imag = transform(spec_real, spec_imag, 1, False)
    spec_real, spec_imag = side_by_side((spec_real, spec_imag), "slab", 1, 0, 2)
    spec_real, spec_imag = transform(spec_real, spec_imag, 0, False)
    count_z = spec_real.shape[0]
    kernel = hartree_kernel(
        jnp.arange(count_z, dtype=jnp.int32),
        count_z,
        slab_id * spec_real.shape[1] + jnp.arange(spec_real.shape[1], dtype=jnp.int32),
        NX,
        sub_id * spec_real.shape[2] + jnp.arange(spec_real.shape[2], dtype=jnp.int32),
        NY,
    )
    spec_real, spec_imag = transform(spec_real * kernel, spec_imag * kernel, 0, True)
    spec_real, spec_imag = side_by_side((spec_real, spec_imag), "slab", 0, 1, 2)
    spec_real, spec_imag = transform(spec_real, spec_imag, 1, True)
    spec_real, spec_imag = side_by_side((spec_real, spec_imag), "sub", 1, 2, 0)
    hartree = apply_axis(spec_real, cosine_table, 2) - apply_axis(spec_imag, sine_table, 2)
    potential = hartree + exchange_correlation(density)
    whole = gathered_copies(potential, "sub", 1)
    widened = jnp.concatenate([whole, whole[:, :BOX]], axis=1)
    widened = jnp.concatenate([widened, widened[:, :, :BOX]], axis=2)

    def cut_window(distance):
        target = (slab_id - distance) % slab_count * sub_count + sub_id
        window = lax.dynamic_slice(
            widened, (0, corners[target, 1], corners[target, 2]), (Z_DEV, BOX, BOX)
        )
        return window.reshape(Z_DEV, BOX * BOX)

    windows = lax.map(cut_window, jnp.arange(reach, dtype=jnp.int32))
    returned = [windows[distance] for distance in range(reach)]
    for level in range((reach - 1).bit_length()):
        chosen = [distance for distance in range(reach) if distance >> level & 1]
        shipped = passed_along(
            jnp.stack([returned[distance] for distance in chosen]), "slab", -(1 << level)
        )
        for position, distance in enumerate(chosen):
            returned[distance] = shipped[position]
    gathered_planes = jnp.stack(returned).reshape(reach * Z_DEV, BOX * BOX)
    box_values = lax.dynamic_slice_in_dim(gathered_planes, plane_offset, BOX, 0)
    return (box_values.reshape(1, BOX * BOX * BOX), potential)


def solution(mesh):
    placed = (
        P(("slab", "sub"), None, None),
        P(("slab", "sub"), None),
        P(("slab", "sub")),
        P(),
        P(("slab", "sub"), None),
        P("slab", "sub", None),
    )
    return jax.shard_map(
        body,
        mesh=mesh,
        in_specs=placed,
        out_specs=(P(("slab", "sub"), None), P("slab", "sub", None)),
        check_vma=False,
    )
```

profile of v0, /device:TPU:24, one launch (start us, length us, event | category | flops | bytes accessed | tf_op | source)
XLA Modules:
  0.0 494.1 jit_solution(12894519837613981728)
XLA Ops:
  18.9 12.0 %collective-permute-done = f32[6,4,2304]{2,1,0:T(4,128)S(1)} collective-permute-done((f32[6,4,2304]{2,1,0:T(4,128)S(1)}, f32[6,4,2304]{2,1,0:T(4,128)S(1)}, u32[]{:S(2)}, u32[]{:S(2)}) %collective-permute-start) | collective-permute-done | bytes 221216 | tf_op jit(solution)/shard_map/ppermute | solution.py:20
  32.9 8.0 %collective-permute-done.1 = f32[6,4,2304]{2,1,0:T(4,128)S(1)} collective-permute-done((f32[6,4,2304]{2,1,0:T(4,128)S(1)}, f32[6,4,2304]{2,1,0:T(4,128)S(1)}, u32[]{:S(2)}, u32[]{:S(2)}) %collective-permute-start.1) | collective-permute-done | bytes 221216 | tf_op jit(solution)/shard_map/ppermute | solution.py:20
  42.9 9.7 %collective-permute-done.2 = f32[5,4,2304]{2,1,0:T(4,128)S(1)} collective-permute-done((f32[5,4,2304]{2,1,0:T(4,128)S(1)}, f32[5,4,2304]{2,1,0:T(4,128)S(1)}, u32[]{:S(2)}, u32[]{:S(2)}) %collective-permute-start.2) | collective-permute-done | bytes 184352 | tf_op jit(solution)/shard_map/ppermute | solution.py:20
  52.6 6.1 %collective-permute-start.3 = (f32[5,4,2304]{2,1,0:T(4,128)S(1)}, f32[5,4,2304]{2,1,0:T(4,128)S(1)}, u32[]{:S(2)}, u32[]{:S(2)}) collective-permute-start(f32[5,4,2304]{2,1,0:T(4,128)S(1)} %pad_maximum_fusion.6), channel_id=1, source_target_pairs={{0,32},{4,36},{8,40},{12,44},{16,48},{20,52},{24,56},{28,60},{32,6... | collective-permute-start | bytes 552968 | tf_op jit(solution)/shard_map/ppermute | solution.py:20
  58.8 7.6 %collective-permute-done.3 = f32[5,4,2304]{2,1,0:T(4,128)S(1)} collective-permute-done((f32[5,4,2304]{2,1,0:T(4,128)S(1)}, f32[5,4,2304]{2,1,0:T(4,128)S(1)}, u32[]{:S(2)}, u32[]{:S(2)}) %collective-permute-start.3) | collective-permute-done | bytes 184352 | tf_op jit(solution)/shard_map/ppermute | solution.py:20
  66.5 101.0 %while.27 = (s32[]{:T(128)}, f32[4,304,304]{2,1,0:T(8,128)S(1)}, s32[]{:T(128)}, s32[]{:T(128)}, s32[512,3]{0,1:T(4,128)}, /*index=5*/f32[13,4,2304]{2,1,0:T(4,1...) while((s32[]{:T(128)}, f32[4,304,304]{2,1,0:T(8,128)S(1)}, ...), condition=%wide.region_2.3_spmd, body=%wide.region_1.2_spmd.sunk | while | flops 9241 | bytes 332184 | solution.py:153
  167.8 15.1 %all_to_all.76 = f32[4,4,64,256]{3,2,1,0:T(8,128)S(1)} all-to-all(f32[4,4,64,256]{3,2,1,0:T(8,128)S(1)} %copy.40), channel_id=1, replica_groups=mesh['slab'=128,'sub'=4] {'sub'}, dimensions={0} | all-to-all | bytes 2097152 | tf_op jit(solution)/shard_map/all_to_all | solution.py:31
  186.8 10.7 %all_to_all.77 = f32[4,1,32768]{2,1,0:T(1,128)S(1)} all-to-all(f32[4,1,32768]{2,1,0:T(1,128)S(1)} %reshape.217), channel_id=1, replica_groups=mesh['slab'=128,'sub'=4] {'sub'}, dimensions={0} | all-to-all | bytes 1048576 | tf_op jit(solution)/shard_map/all_to_all | solution.py:38
  208.7 15.0 %all-to-all-start.2 = ((f32[4,256,128]{2,0,1:T(4,128)}), f32[4,256,128]{2,0,1:T(4,128)S(1)}, u32[]{:S(2)}, u32[]{:S(2)}) async-start(f32[4,256,128]{2,0,1:T(4,128)} %copy.43), calls=%async_computation.2 | async-start | bytes 1048576 | tf_op jit(solution)/shard_map/all_to_all | solution.py:38
  223.8 18.2 %all-to-all-done.2 = f32[4,256,128]{2,0,1:T(4,128)S(1)} async-done(((f32[4,256,128]{2,0,1:T(4,128)}), f32[4,256,128]{2,0,1:T(4,128)S(1)}, u32[]{:S(2)}, u32[]{:S(2)}) %all-to-all-start.2) | async-done | bytes 524320 | tf_op jit(solution)/shard_map/all_to_all | solution.py:38
  242.8 5.3 %fusion.29 = f32[512,128]{0,1:S(1)} fusion(f32[512,128]{0,1:T(8,128)S(1)} %bitcast.194), kind=kOutput, calls=%fused_computation.48 | convolution fusion | flops 406323200 | bytes 524288
  248.0 5.2 %fusion.17 = f32[512,128]{0,1:S(1)} fusion(f32[512,128]{0,1:T(8,128)S(1)} %bitcast.195), kind=kOutput, calls=%fused_computation.42 | convolution fusion | flops 406323200 | bytes 524288
  258.7 5.3 %fusion.27 = f32[512,128]{0,1:S(1)} fusion(f32[512,128]{0,1:T(8,128)S(1)} %bitcast.197), kind=kOutput, calls=%fused_computation.47 | convolution fusion | flops 406323200 | bytes 524288
  264.2 5.4 %fusion.25 = f32[512,128]{0,1:S(1)} fusion(f32[512,128]{0,1:T(8,128)S(1)} %bitcast.202), kind=kOutput, calls=%fused_computation.46 | convolution fusion | flops 406323200 | bytes 524288
  269.7 5.2 %fusion.15 = f32[512,128]{0,1:S(1)} fusion(f32[512,128]{0,1:T(8,128)S(1)} %bitcast.203), kind=kOutput, calls=%fused_computation.41 | convolution fusion | flops 406323200 | bytes 524288
  274.9 5.2 %fusion.19 = f32[512,128]{0,1:S(1)} fusion(f32[512,128]{0,1:T(8,128)S(1)} %bitcast.200), kind=kOutput, calls=%fused_computation.43 | convolution fusion | flops 406323200 | bytes 524288
  280.2 5.3 %fusion.23 = f32[512,128]{0,1:S(1)} fusion(f32[512,128]{0,1:T(8,128)S(1)} %bitcast.201), kind=kOutput, calls=%fused_computation.45 | convolution fusion | flops 406323200 | bytes 524288
  285.8 26.1 %all_to_all.78 = f32[512,2,128]{2,1,0:T(2,128)S(1)} all-to-all(f32[512,2,128]{2,1,0:T(2,128)S(1)} %copy.48), channel_id=1, replica_groups=mesh['slab'=128,'sub'=4] {'slab'}, dimensions={0} | all-to-all | bytes 1048576 | tf_op jit(solution)/shard_map/all_to_all | solution.py:38
  320.6 12.8 %all_to_all.79 = f32[4,1,32768]{2,1,0:T(1,128)S(1)} all-to-all(f32[4,1,32768]{2,1,0:T(1,128)S(1)} %reshape.219), channel_id=1, replica_groups=mesh['slab'=128,'sub'=4] {'sub'}, dimensions={0} | all-to-all | bytes 1048576 | tf_op jit(solution)/shard_map/all_to_all | solution.py:38
  345.4 14.9 %all-to-all-done.5 = f32[4,4,64,256]{3,2,1,0:T(8,128)S(1)} async-done(((f32[4,4,64,256]{3,2,1,0:T(8,128)}), f32[4,4,64,256]{3,2,1,0:T(8,128)S(1)}, u32[]{:S(2)}, u32[]{:S(2)}) %all-to-all-start.5) | async-done | bytes 1048608 | tf_op jit(solution)/shard_map/all_to_all | solution.py:44
  360.5 86.5 %while.28 = (s32[]{:T(128)}, f32[13,4,2304]{2,1,0:T(4,128)S(1)}, s32[13]{0:T(128)S(1)}, s32[]{:T(128)}, s32[]{:T(128)}, /*index=5*/s32[512,3]{0,1:T(4,128)}, f32...) while((s32[]{:T(128)}, f32[13,4,2304]{2,1,0:T(4,128)S(1)}, ...), condition=%wide.region_5.6_spmd, body=%wide.region_4.5_spmd.sunk | while | flops 25 | bytes 221608 | solution.py:194
  455.8 6.8 %collective-permute-done.5 = f32[6,4,2304]{2,1,0:T(4,128)S(1)} collective-permute-done((f32[6,4,2304]{2,1,0:T(4,128)S(1)}, f32[6,4,2304]{2,1,0:T(4,128)S(1)}, u32[]{:S(2)}, u32[]{:S(2)}) %collective-permute-start.5) | collective-permute-done | bytes 221216 | tf_op jit(solution)/shard_map/ppermute | solution.py:20
  464.6 11.9 %collective-permute-done.6 = f32[5,4,2304]{2,1,0:T(4,128)S(1)} collective-permute-done((f32[5,4,2304]{2,1,0:T(4,128)S(1)}, f32[5,4,2304]{2,1,0:T(4,128)S(1)}, u32[]{:S(2)}, u32[]{:S(2)}) %collective-permute-start.6) | collective-permute-done | bytes 184352 | tf_op jit(solution)/shard_map/ppermute | solution.py:20
  479.0 13.3 %collective-permute-done.7 = f32[5,4,2304]{2,1,0:T(4,128)S(1)} collective-permute-done((f32[5,4,2304]{2,1,0:T(4,128)S(1)}, f32[5,4,2304]{2,1,0:T(4,128)S(1)}, u32[]{:S(2)}, u32[]{:S(2)}) %collective-permute-start.7) | collective-permute-done | bytes 184352 | tf_op jit(solution)/shard_map/ppermute | solution.py:20
  (259 shorter events, 153.7 us)
Async XLA Ops:
  17.0 13.9 %collective-permute-start = (f32[6,4,2304]{2,1,0:T(4,128)S(1)}, f32[6,4,2304]{2,1,0:T(4,128)S(1)}, u32[]{:S(2)}, u32[]{:S(2)}) collective-permute-start(f32[6,4,2304]{2,1,0:T(4,128)S(1)} %get-tuple-element.291), channel_id=1, source_target_pairs={{0,4},{4,8},{8,12},{12,16},{16,20},{20,24},{24,28},{28,32},{32,36}... | collective-permute-start | bytes 663560 | tf_op jit(solution)/shard_map/ppermute | solution.py:20
  31.0 9.9 %collective-permute-start.1 = (f32[6,4,2304]{2,1,0:T(4,128)S(1)}, f32[6,4,2304]{2,1,0:T(4,128)S(1)}, u32[]{:S(2)}, u32[]{:S(2)}) collective-permute-start(f32[6,4,2304]{2,1,0:T(4,128)S(1)} %get-tuple-element.308), channel_id=1, source_target_pairs={{0,8},{4,12},{8,16},{12,20},{16,24},{20,28},{24,32},{28,36},{32,40... | collective-permute-start | bytes 663560 | tf_op jit(solution)/shard_map/ppermute | solution.py:20
  41.0 11.6 %collective-permute-start.2 = (f32[5,4,2304]{2,1,0:T(4,128)S(1)}, f32[5,4,2304]{2,1,0:T(4,128)S(1)}, u32[]{:S(2)}, u32[]{:S(2)}) collective-permute-start(f32[5,4,2304]{2,1,0:T(4,128)S(1)} %pad_maximum_fusion.5), channel_id=1, source_target_pairs={{0,16},{4,20},{8,24},{12,28},{16,32},{20,36},{24,40},{28,44},{32,4... | collective-permute-start | bytes 552968 | tf_op jit(solution)/shard_map/ppermute | solution.py:20
  52.6 13.7 %collective-permute-start.3 = (f32[5,4,2304]{2,1,0:T(4,128)S(1)}, f32[5,4,2304]{2,1,0:T(4,128)S(1)}, u32[]{:S(2)}, u32[]{:S(2)}) collective-permute-start(f32[5,4,2304]{2,1,0:T(4,128)S(1)} %pad_maximum_fusion.6), channel_id=1, source_target_pairs={{0,32},{4,36},{8,40},{12,44},{16,48},{20,52},{24,56},{28,60},{32,6... | collective-permute-start | bytes 552968 | tf_op jit(solution)/shard_map/ppermute | solution.py:20
  167.8 15.2 %copy-start.1 = (f32[4,64,256]{2,1,0:T(8,128)S(1)}, f32[4,64,256]{2,1,0:T(8,128)}, u32[]{:S(2)}) copy-start(f32[4,64,256]{2,1,0:T(8,128)} %param.15) | copy-start | bytes 786436
  208.7 33.3 %all-to-all-start.2 = ((f32[4,256,128]{2,0,1:T(4,128)}), f32[4,256,128]{2,0,1:T(4,128)S(1)}, u32[]{:S(2)}, u32[]{:S(2)}) async-start(f32[4,256,128]{2,0,1:T(4,128)} %copy.43), calls=%async_computation.2 | async-start | bytes 1048576 | tf_op jit(solution)/shard_map/all_to_all | solution.py:38
  340.8 19.6 %copy-start = (f32[4,64,256]{2,1,0:T(8,128)}, f32[4,64,256]{2,1,0:T(8,128)S(1)}, u32[]{:S(2)}) copy-start(f32[4,64,256]{2,1,0:T(8,128)S(1)} %fusion.2) | copy-start | bytes 786436
  341.9 18.4 %all-to-all-start.5 = ((f32[4,4,64,256]{3,2,1,0:T(8,128)}), f32[4,4,64,256]{3,2,1,0:T(8,128)S(1)}, u32[]{:S(2)}, u32[]{:S(2)}) async-start(f32[4,4,64,256]{3,2,1,0:T(8,128)} %broadcast_in_dim.23), calls=%async_computation.5 | async-start | bytes 2097152 | tf_op jit(solution)/shard_map/all_to_all | solution.py:44
  447.1 5.4 %collective-permute-start.4 = (f32[6,4,2304]{2,1,0:T(4,128)S(1)}, f32[6,4,2304]{2,1,0:T(4,128)S(1)}, u32[]{:S(2)}, u32[]{:S(2)}) collective-permute-start(f32[6,4,2304]{2,1,0:T(4,128)S(1)} %get-tuple-element.298), channel_id=1, source_target_pairs={{0,508},{4,0},{8,4},{12,8},{16,12},{20,16},{24,20},{28,24},{32,28}... | collective-permute-start | bytes 663560 | tf_op jit(solution)/shard_map/ppermute | solution.py:20
  452.6 10.0 %collective-permute-start.5 = (f32[6,4,2304]{2,1,0:T(4,128)S(1)}, f32[6,4,2304]{2,1,0:T(4,128)S(1)}, u32[]{:S(2)}, u32[]{:S(2)}) collective-permute-start(f32[6,4,2304]{2,1,0:T(4,128)S(1)} %get-tuple-element.301), channel_id=1, source_target_pairs={{0,504},{4,508},{8,0},{12,4},{16,8},{20,12},{24,16},{28,20},{32,24... | collective-permute-start | bytes 663560 | tf_op jit(solution)/shard_map/ppermute | solution.py:20
  462.7 13.9 %collective-permute-start.6 = (f32[5,4,2304]{2,1,0:T(4,128)S(1)}, f32[5,4,2304]{2,1,0:T(4,128)S(1)}, u32[]{:S(2)}, u32[]{:S(2)}) collective-permute-start(f32[5,4,2304]{2,1,0:T(4,128)S(1)} %pad_maximum_fusion.7), channel_id=1, source_target_pairs={{0,496},{4,500},{8,504},{12,508},{16,0},{20,4},{24,8},{28,12},{32,... | collective-permute-start | bytes 552968 | tf_op jit(solution)/shard_map/ppermute | solution.py:20
  476.6 15.7 %collective-permute-start.7 = (f32[5,4,2304]{2,1,0:T(4,128)S(1)}, f32[5,4,2304]{2,1,0:T(4,128)S(1)}, u32[]{:S(2)}, u32[]{:S(2)}) collective-permute-start(f32[5,4,2304]{2,1,0:T(4,128)S(1)} %pad_maximum_fusion.8), channel_id=1, source_target_pairs={{0,480},{4,484},{8,488},{12,492},{16,496},{20,500},{24,504},{28,50... | collective-permute-start | bytes 552968 | tf_op jit(solution)/shard_map/ppermute | solution.py:20
where the time goes:
time: 504 us; the launch traced here: 494 us
  loops' own time  108 us (21%)
  waiting for transfers between devices  106 us (21%)
  local copies, waits for them, and re-layouts  94.9 us (19%)
  blocking collectives  64.7 us (13%)
  matrix products  60.7 us (12%)
  starting transfers between devices  39.7 us (8%)
  other arithmetic  13 us (3%)
  between operations  7.02 us (1%)
    ppermute x8, waiting for transfers between devices, passed_along(): lax.ppermute(shard, axis, [(i, (i + by) % length) for i in range(length)])  72.6 us
    another operation x1, loops' own time, body(): windows = lax.map(cut_window, jnp.arange(reach, dtype=jnp.int32))  57.8 us
    another operation x1, loops' own time, body(): lax.fori_loop(0, reach, place_piece, jnp.zeros((Z_DEV, NX + BOX, NY + BOX...  50.6 us
    all_to_all x3, blocking collectives, side_by_side(): lax.all_to_all(both, axis, split_axis=split_dim, concat_axis=concat_dim,...  49.6 us
    unnamed x8, matrix products  42.3 us
    dynamic_update_slice x13, local copies, waits for them, and re-layouts, place_piece(): lax.dynamic_update_slice(frame, current + piece, (0, start_x, start_y))  29.8 us
    ppermute x8, starting transfers between devices, passed_along(): lax.ppermute(shard, axis, [(i, (i + by) % length) for i in range(length)])  21.2 us
    all_to_all x1, waiting for transfers between devices, side_by_side(): lax.all_to_all(both, axis, split_axis=split_dim, concat_axis=concat_dim,...  18.2 us
  transfers between devices with their start and end apart: 10, of which 10 were waited for; matrix products, arithmetic and copies ran while one was open for 0% of the time, Pallas kernels for 0%

commit v1 on v0

v1 whole, which is shorter than its diff:
```python
import functools
import math

import jax
import jax.numpy as jnp
import numpy as np
from jax import lax
from jax.experimental import pallas as pl
from jax.experimental.pallas import tpu as pltpu
from jax.sharding import PartitionSpec as P

BOX = 48
NX = 256
NY = 256
Z_DEV = 4
SUBS = 4
CORE = 32
FIRST = 8
SPACING = 0.35
FLOOR = 0.001
NEAR = FIRST // Z_DEV
REACH = 11
SPREAD = 13
TILES = BOX * BOX // 128
MESH = pl.DeviceIdType.MESH
f32 = jnp.float32
bf16 = jnp.bfloat16


def cas_table(count):
    index = np.arange(count)
    angle = 2.0 * np.pi * ((index[:, None] * index[None, :]) % count) / count
    table = (np.cos(angle) + np.sin(angle)) / np.sqrt(count)
    high = table.astype(np.float32).astype(bf16)
    low = (table - high.astype(np.float64)).astype(np.float32).astype(bf16)
    return high, low


def split(values):
    high = values.astype(bf16)
    return high, (values - high.astype(f32)).astype(bf16)


def dot(a, b):
    return jnp.dot(a, b, preferred_element_type=f32)


def dot3(a, b):
    return dot(a[0], b[0]) + (dot(a[0], b[1]) + dot(a[1], b[0]))


def lanes(shape):
    return lax.broadcasted_iota(jnp.int32, shape, len(shape) - 1)


def rows(shape):
    return lax.broadcasted_iota(jnp.int32, shape, 0)


def core_kernel(span_ref, corner_ref, box_ref, core_ref, meta_ref):
    slab = lax.axis_index("slab")
    own = slab * SUBS + lax.axis_index("sub")
    first_z, first_x, first_y = span_ref[0], span_ref[1], span_ref[2]
    long_z, long_x, long_y = span_ref[3], span_ref[4], span_ref[5]
    offset = corner_ref[own * 3] - slab * Z_DEV
    planes = BOX - FIRST
    start = first_x * BOX + first_y
    tile, lane = start // 128, start % 128
    shape = (planes, 128)
    column = lanes(shape)
    turned = []
    for t in range(13):
        row = FIRST * TILES + jnp.minimum(tile + t, TILES - 1)
        raw = box_ref[pl.ds(row, planes, stride=TILES), :]
        turned.append(pltpu.roll(raw, (128 - lane) % 128, 1))
    chunks = [jnp.where(column < 128 - lane, turned[t], turned[t + 1]) for t in range(12)]
    plane = rows(shape) + FIRST
    within_z = (plane >= first_z) & (plane < first_z + long_z)
    core_ref[...] = jnp.zeros_like(core_ref)
    for t in range(8):
        value = jnp.zeros(shape, f32)
        for m in range(4):
            source = (4 * t + m) * BOX
            chunk, begin = source // 128, source % 128
            shift = (32 * m - begin) % 128
            piece = pltpu.roll(chunks[chunk], shift, 1)
            if begin + CORE > 128:
                after = pltpu.roll(chunks[chunk + 1], shift, 1)
                piece = jnp.where(column < 32 * m + 128 - begin, piece, after)
            value = jnp.where(column // 32 == m, piece, value)
        inside = within_z & (4 * t + column // 32 < long_x) & (column % 32 < long_y)
        core_ref[pl.ds(offset * 8 + t, planes, stride=8), :] = jnp.where(inside, value, 0.0)
    start_x = (corner_ref[own * 3 + 1] + first_x) % NX
    start_y = (corner_ref[own * 3 + 2] + first_y) % NY
    meta_ref[...] = jnp.where(lanes((8, 128)) == 0, start_x, start_y)


def wait_all(sem, ref):
    pltpu.make_async_copy(ref, ref, sem).wait()


def spread_kernel(core_ref, meta_ref, outer_ref, got_ref, told_ref, plane_ref, send, recv):
    slab, sub = lax.axis_index("slab"), lax.axis_index("sub")
    slabs = lax.axis_size("slab")

    def pass_outer(k, carry):
        target = (sub + k) % SUBS
        pltpu.make_async_remote_copy(
            outer_ref.at[target],
            plane_ref.at[pl.ds(sub * 64, 64)],
            send.at[2],
            recv.at[2],
            device_id=(slab, target),
            device_id_type=MESH,
        ).start()
        return carry

    def pass_core(p, carry):
        target = (slab + NEAR + p // SUBS) % slabs
        pltpu.make_async_remote_copy(
            core_ref.at[pl.ds(p * 8, 8)],
            got_ref.at[pl.ds((p // SUBS * SUBS + sub) * 8, 8)],
            send.at[0],
            recv.at[0],
            device_id=(target, p % SUBS),
            device_id_type=MESH,
        ).start()
        return carry

    def pass_meta(d, carry):
        pltpu.make_async_remote_copy(
            meta_ref.at[pl.ds(0, 1)],
            told_ref.at[pl.ds(d, 1)],
            send.at[1],
            recv.at[1],
            device_id=((slab + NEAR + d) % slabs, sub),
            device_id_type=MESH,
        ).start()
        return carry

    lax.fori_loop(0, REACH, pass_meta, 0)
    lax.fori_loop(0, REACH * SUBS, pass_core, 0)
    lax.fori_loop(1, SUBS, pass_outer, 0)
    plane_ref[pl.ds(pl.multiple_of(sub * 64, 64), 64), :] = outer_ref[sub]
    for sem in (send, recv):
        wait_all(sem.at[0], got_ref)
        wait_all(sem.at[1], told_ref)
        wait_all(sem.at[2], plane_ref.at[pl.ds(0, 192)])


def forward_kernel(told_ref, got_ref, plane_ref, high_ref, low_ref, density_ref, spec_ref, wide, part):
    for half in range(2):
        wide[half, pl.ds(0, NX), :] = plane_ref[:, pl.ds(half * 128, 128)]
        wide[half, pl.ds(NX, CORE), :] = jnp.zeros((CORE, 128), f32)
    column = lanes((8, 128))

    def place(d, carry):
        base = pl.multiple_of(d * 32, 32)
        cells = got_ref[pl.ds(base, 8), :]
        for q in range(1, SUBS):
            cells = cells + got_ref[pl.ds(base + 8 * q, 8), :]
        start_x, start_y = told_ref[d, 0], told_ref[d, 1]
        for m in range(4):
            piece = pltpu.roll(cells, (128 - 32 * m) % 128, 1)
            piece = jnp.where(column < 32, piece, 0.0)
            piece = jnp.concatenate([piece, jnp.zeros((8, 128), f32)], axis=1)
            piece = pltpu.roll(piece, start_y, 1)
            part[0, pl.ds(m, 8, stride=4), :] = piece[:, :128]
            part[1, pl.ds(m, 8, stride=4), :] = piece[:, 128:]
        here = pl.ds(start_x, CORE)
        for half in range(2):
            wide[half, here, :] = wide[half, here, :] + part[half]
        return carry

    lax.fori_loop(0, REACH, place, 0)
    for half in range(2):
        again = wide[half, pl.ds(NX, CORE), :]
        wide[half, pl.ds(0, CORE), :] = wide[half, pl.ds(0, CORE), :] + again
    density = jnp.concatenate([wide[half, pl.ds(0, NX), :] for half in range(2)], axis=1)
    density_ref[...] = density
    table = (high_ref[...], low_ref[...])
    spec = dot3(table, split(dot3(split(density), table)))
    spec_ref[pl.ds(0, NX), :] = spec[:, :128]
    spec_ref[pl.ds(NX, NX), :] = spec[:, 128:]


def to_everyone(src, dst, me, count, send, recv):
    def one(i, carry):
        target = (me + i) % count
        pltpu.make_async_remote_copy(
            src.at[pl.ds(target, 1)],
            dst.at[pl.ds(me, 1)],
            send,
            recv,
            device_id=(target // SUBS, target % SUBS),
            device_id_type=MESH,
        ).start()
        return carry

    lax.fori_loop(1, count, one, 0)
    dst[pl.ds(me, 1), :] = src[pl.ds(me, 1), :]
    wait_all(recv, dst.at[pl.ds(0, count - 1)])


def wave_squares(index, count):
    folded = jnp.where(index > count // 2, index - count, index)
    wave = (2.0 * math.pi / (count * SPACING)) * folded.astype(f32)
    return wave * wave


def z_kernel(spec_ref, high_ref, low_ref, back_ref, got, turned, send, recv):
    count = lax.axis_size("slab") * SUBS
    me = lax.axis_index("slab") * SUBS + lax.axis_index("sub")
    to_everyone(spec_ref, got, me, count, send.at[0], recv.at[0])
    table = (high_ref[...], low_ref[...])
    values = dot3(table, split(got[...]))
    shape = (count, 128)
    square = (
        wave_squares(rows(shape), count)
        + wave_squares(jnp.zeros(shape, jnp.int32) + me % NX, NX)
        + wave_squares(lanes(shape) + me // NX * 128, NY)
    )
    factor = jnp.where(square > 0, 4.0 * math.pi / jnp.where(square > 0, square, 1.0), 0.0)
    turned[...] = dot3(table, split(values * factor))
    to_everyone(turned, back_ref, me, count, send.at[1], recv.at[1])
    for k in range(2):
        wait_all(send.at[k], back_ref.at[pl.ds(0, count - 1)])


def exchange_correlation(density):
    clipped = jnp.maximum(density, FLOOR)
    root = jnp.exp(jnp.log(clipped) * (1.0 / 3.0))
    radius = (3.0 / (4.0 * math.pi)) ** (1.0 / 3.0) / root
    exchange = -((3.0 / math.pi) ** (1.0 / 3.0)) * root
    inverse = 1.0 / (radius + 7.8)
    return exchange - 0.44 * inverse - (0.44 / 3.0) * radius * inverse * inverse


def inverse_kernel(corner_ref, back_ref, density_ref, high_ref, low_ref, potential_ref, window_ref, wide, cut):
    slab = lax.axis_index("slab")
    slabs = lax.axis_size("slab")
    table = (high_ref[...], low_ref[...])
    spec = jnp.concatenate([back_ref[pl.ds(0, NX), :], back_ref[pl.ds(NX, NX), :]], axis=1)
    hartree = dot3(split(dot3(table, split(spec))), table)
    potential = hartree + exchange_correlation(density_ref[...])
    potential_ref[...] = potential
    for half in range(2):
        side = potential[:, half * 128 : half * 128 + 128]
        wide[half, pl.ds(0, NX), :] = side
        wide[half, pl.ds(NX, BOX), :] = side[:BOX]

    def cut_one(k, carry):
        fragment = (slab - k // SUBS + slabs) % slabs * SUBS + k % SUBS
        start_x, start_y = corner_ref[fragment * 3 + 1], corner_ref[fragment * 3 + 2]
        here = pl.ds(start_x, BOX)
        strip = jnp.concatenate([wide[0, here, :], wide[1, here, :]], axis=1)
        strip = pltpu.roll(strip, (NY - start_y) % NY, 1)
        cut[pl.ds(pl.multiple_of(k * BOX, BOX), BOX), :] = strip[:, :128]
        return carry

    lax.fori_loop(0, SPREAD * SUBS, cut_one, 0)
    column = lanes((24, 128))

    def pack(k, carry):
        out = [jnp.zeros((24, 128), f32) for _ in range(3)]
        for b in range(8):
            tile, begin = b * BOX // 128, b * BOX % 128
            value = pltpu.roll(cut[pl.ds(k * 192 + b, 24, stride=8), :], begin, 1)
            here = (column >= begin) & (column < begin + BOX)
            out[tile] = jnp.where(here, value, out[tile])
            if begin + BOX > 128:
                out[tile + 1] = jnp.where(column < begin + BOX - 128, value, out[tile + 1])
        for t in range(3):
            window_ref[pl.ds(k * 72 + t, 24, stride=3), :] = out[t]
        return carry

    lax.fori_loop(0, SPREAD, pack, 0)


def gather_kernel(window_ref, potential_ref, frame_ref, out_ref, send, recv):
    slab, sub = lax.axis_index("slab"), lax.axis_index("sub")
    slabs = lax.axis_size("slab")

    def pass_window(k, carry):
        @pl.when(k != sub)
        def _():
            pltpu.make_async_remote_copy(
                window_ref.at[pl.ds(k * TILES, TILES)],
                frame_ref.at[pl.ds((k // SUBS * SUBS + sub) * TILES, TILES)],
                send.at[0],
                recv.at[0],
                device_id=((slab - k // SUBS + slabs) % slabs, k % SUBS),
                device_id_type=MESH,
            ).start()

        return carry

    def pass_plane(k, carry):
        target = (sub + k) % SUBS
        pltpu.make_async_remote_copy(
            potential_ref.at[pl.ds(target * 64, 64)],
            out_ref.at[sub],
            send.at[1],
            recv.at[1],
            device_id=(slab, target),
            device_id_type=MESH,
        ).start()
        return carry

    lax.fori_loop(0, SPREAD * SUBS, pass_window, 0)
    lax.fori_loop(1, SUBS, pass_plane, 0)
    frame_ref[pl.ds(sub * TILES, TILES), :] = window_ref[pl.ds(sub * TILES, TILES), :]
    out_ref[sub] = potential_ref[pl.ds(pl.multiple_of(sub * 64, 64), 64), :]
    for sem in (send, recv):
        wait_all(sem.at[0], frame_ref.at[pl.ds(0, (SPREAD * SUBS - 1) * TILES)])
        wait_all(sem.at[1], out_ref.at[pl.ds(0, SUBS - 1)])


def call(kernel, shapes, smem=0, count=0, scratch=(), remote=False, name=None):
    in_specs = [pl.BlockSpec(memory_space=pltpu.SMEM)] * smem + [
        pl.BlockSpec(memory_space=pltpu.VMEM)
    ] * (count - smem)
    return pl.pallas_call(
        kernel,
        out_shape=[jax.ShapeDtypeStruct(s, t) for s, t in shapes],
        in_specs=in_specs,
        out_specs=[pl.BlockSpec(memory_space=pltpu.VMEM)] * len(shapes),
        scratch_shapes=list(scratch),
        compiler_params=pltpu.CompilerParams(has_side_effects=remote),
        name=name,
    )


def body(orbitals, occupations, patch_sign, corners, core_span, outer_density):
    slab_id = lax.axis_index("slab")
    own = slab_id * SUBS + lax.axis_index("sub")
    count = lax.axis_size("slab") * SUBS
    flat_corners = corners.reshape(-1)
    weights = occupations[0].astype(f32) * patch_sign[0].astype(f32)
    box = jnp.sum(weights[:, None] * jnp.square(orbitals[0].astype(f32)), axis=0)
    sems = [pltpu.SemaphoreType.DMA((3,)), pltpu.SemaphoreType.DMA((3,))]
    core, meta = call(
        core_kernel, [((REACH * SUBS * 8, 128), f32), ((8, 128), jnp.int32)], 2, 3, name="core"
    )(core_span[0], flat_corners, box.reshape(BOX * TILES, 128))
    got, told, plane = call(
        spread_kernel,
        [((REACH * SUBS * 8, 128), f32), ((REACH, 128), jnp.int32), ((NX, NY), f32)],
        0,
        3,
        sems,
        True,
        name="spread",
    )(core, meta, outer_density)
    plane_table = [jnp.asarray(t) for t in cas_table(NX)]
    z_table = [jnp.asarray(t) for t in cas_table(count)]
    density, spec = call(
        forward_kernel,
        [((NX, NY), f32), ((count, 128), f32)],
        1,
        5,
        [pltpu.VMEM((2, NX + CORE, 128), f32), pltpu.VMEM((2, CORE, 128), f32)],
        name="forward",
    )(told, got, plane, *plane_table)
    (back,) = call(
        z_kernel,
        [((count, 128), f32)],
        0,
        3,
        [pltpu.VMEM((count, 128), f32), pltpu.VMEM((count, 128), f32), *sems],
        True,
        name="along_z",
    )(spec, *z_table)
    potential, windows = call(
        inverse_kernel,
        [((NX, NY), f32), ((SPREAD * SUBS * TILES, 128), f32)],
        1,
        5,
        [pltpu.VMEM((2, NX + BOX, 128), f32), pltpu.VMEM((SPREAD * SUBS * BOX, 128), f32)],
        name="inverse",
    )(flat_corners, back, density, *plane_table)
    frame, out = call(
        gather_kernel,
        [((SPREAD * SUBS * TILES, 128), f32), ((Z_DEV, NX // SUBS, NY), f32)],
        0,
        2,
        sems,
        True,
        name="gather",
    )(windows, potential)
    offset = corners[own, 0] - slab_id * Z_DEV
    planes = lax.dynamic_slice(frame, (offset * TILES, 0), (BOX * TILES, 128))
    return planes.reshape(1, BOX * BOX * BOX), out


def solution(mesh):
    placed = (
        P(("slab", "sub"), None, None),
        P(("slab", "sub"), None),
        P(("slab", "sub")),
        P(),
        P(("slab", "sub"), None),
        P("slab", "sub", None),
    )
    return jax.shard_map(
        body,
        mesh=mesh,
        in_specs=placed,
        out_specs=(P(("slab", "sub"), None), P("slab", "sub", None)),
        check_vma=False,
    )
```

time: 504 us -> 154 us (0.31)
  the two profiles are of different devices: /device:TPU:24 before, /device:TPU:56 now
where the time goes in v1:
time: 154 us; the launch traced here: 152 us
  Pallas kernels  139 us (90%)
  local copies, waits for them, and re-layouts  6.41 us (4%)
  other arithmetic  5.16 us (3%)
  between operations  1.98 us (1%)
    pallas_call x1, Pallas kernels, body(): call(z_kernel, [((count, 128), f32)], 0, 3, [pltpu.VMEM((count, 128), f32...  49.6 us
    pallas_call x1, Pallas kernels, body(): call(gather_kernel, [((SPREAD * SUBS * TILES, 128), f32), ((Z_DEV, NX //...  40 us
    pallas_call x1, Pallas kernels, body(): call(spread_kernel, [((REACH * SUBS * 8, 128), f32), ((REACH, 128), jnp.i...  34.9 us
    pallas_call x1, Pallas kernels, body(): call(inverse_kernel, [((NX, NY), f32), ((SPREAD * SUBS * TILES, 128), f32...  8.11 us
    reduce_sum x1, other arithmetic, body(): jnp.sum(weights[:, None] * jnp.square(orbitals[0].astype(f32)), axis=0)  4.5 us
    pallas_call x1, Pallas kernels, body(): call(forward_kernel, [((NX, NY), f32), ((count, 128), f32)], 1, 5, [pltpu...  4.21 us

profile of v1, /device:TPU:56, one launch (start us, length us, event | category | flops | bytes accessed | tf_op | source)
XLA Modules:
  0.0 152.3 jit_solution(12747669047048101658)
XLA Ops:
  0.6 0.8 copy.12
  1.5 0.8 reshape.25.corner_ref
  2.9 0.7 multiply_bitcast_fusion
  3.6 4.5 %fusion = f32[110592]{0:T(1024)} fusion(bf16[1,16,110592]{2,1,0:T(8,128)(2,1)} %param.10, f32[16]{0:T(128)S(1)} %multiply_bitcast_fusion), kind=kLoop, calls=%fused_computation.1 | loop fusion | flops 6967296 | bytes 3981376 | tf_op jit(solution)/shard_map/reduce_sum | solution.py:340
  8.1 2.0 %core.1 = (f32[352,128]{1,0:T(8,128)}, s32[8,128]{1,0:T(8,128)}) custom-call(s32[6]{0:T(128)} %bitcast.13, s32[1536]{0:T(1024)} %reshape.25.corner_ref, f32[864,128]{1,0:T(8,128)} %bitcast.11), custom_call_target="tpu_custom_call" | custom-call | tf_op jit(solution)/shard_map/core/pallas_call | solution.py:342
  10.1 34.9 %spread.1 = (f32[352,128]{1,0:T(8,128)}, s32[11,128]{1,0:T(8,128)}, f32[256,256]{1,0:T(8,128)}) custom-call(f32[352,128]{1,0:T(8,128)} %get-tuple-element.13.core_ref, s32[8,128]{1,0:T(8,128)} %get-tuple-element.14.meta_ref, f32[4,64,256]{2,1,0:T(8,128)} %outer_ref.1), custom_call_target="tpu_custom_call" | custom-call | tf_op jit(solution)/shard_map/spread/pallas_call | solution.py:345
  45.0 4.2 %forward.1 = (f32[256,256]{1,0:T(8,128)}, f32[512,128]{1,0:T(8,128)}) custom-call(s32[11,128]{1,0:T(8,128)} %get-tuple-element.15.told_ref, f32[352,128]{1,0:T(8,128)} %get-tuple-element.16.got_ref, f32[256,256]{1,0:T(8,128)} %get-tuple-element.17.plane_ref, bf16[256,256]{1,0:T(8,128)(2,1)} %constant.29.clone.high_ref, bf16[256,256]{1,0:T(8,128)(2,1)} %constant.30.clone.low_ref), custom_call_target="tpu_custom_call" | custom-call | tf_op jit(solution)/shard_map/forward/pallas_call | solution.py:356
  49.2 49.6 %along_z.1.back_ref = f32[512,128]{1,0:T(8,128)} custom-call(f32[512,128]{1,0:T(8,128)} %get-tuple-element.18.spec_ref, bf16[512,512]{1,0:T(8,128)(2,1)} %constant.31.clone.high_ref, bf16[512,512]{1,0:T(8,128)(2,1)} %constant.32.clone.low_ref), custom_call_target="tpu_custom_call" | custom-call | tf_op jit(solution)/shard_map/along_z/pallas_call | solution.py:364
  98.8 8.1 %inverse.1 = (f32[256,256]{1,0:T(8,128)}, f32[936,128]{1,0:T(8,128)}) custom-call(s32[1536]{0:T(1024)} %reshape.25.corner_ref, f32[512,128]{1,0:T(8,128)} %along_z.1.back_ref, f32[256,256]{1,0:T(8,128)} %get-tuple-element.19.density_ref, bf16[256,256]{1,0:T(8,128)(2,1)} %constant.29.clone.high_ref, bf16[256,256]{1,0:T(8,128)(2,1)} %constant.30.clone.low_ref), custom_call_target="tpu_custom_call" | custom-call | tf_op jit(solution)/shard_map/inverse/pallas_call | solution.py:373
  106.9 40.0 %gather.1 = (f32[936,128]{1,0:T(8,128)}, f32[4,64,256]{2,1,0:T(8,128)}) custom-call(f32[936,128]{1,0:T(8,128)} %get-tuple-element.20.window_ref, f32[256,256]{1,0:T(8,128)} %get-tuple-element.21.potential_ref), custom_call_target="tpu_custom_call" | custom-call | tf_op jit(solution)/shard_map/gather/pallas_call | solution.py:381
  146.9 1.3 constant_dynamic-slice_fusion.1
  148.8 1.8 %constant_dynamic-slice_fusion = f32[864,128]{1,0:T(8,128)} fusion(f32[936,128]{1,0:T(8,128)} %get-tuple-element.22, s32[]{:T(128)S(6)} %select_n.7), kind=kLoop, calls=%fused_computation.2 | loop fusion | bytes 884740 | tf_op jit(solution)/shard_map/dynamic_slice | solution.py:391
  150.7 1.7 %copy.15 = f32[4,64,256]{2,1,0:T(8,128)} copy(f32[4,64,256]{2,1,0:T(8,128)} %get-tuple-element.27) | data formatting | bytes 524288

commit v2 on v0

v2 whole, which is shorter than its diff:
```python
import math

import jax
import jax.numpy as jnp
import numpy as np
from jax import lax
from jax.experimental import pallas as pl
from jax.experimental.pallas import tpu as pltpu
from jax.sharding import PartitionSpec as P

BOX = 48
ORB = 16
NX = 256
NY = 256
Z_DEV = 4
SUBS = 4
CORE = 32
FIRST = 8
SPACING = 0.35
FLOOR = 0.001
NEAR = FIRST // Z_DEV
REACH = 11
SPREAD = 13
TILES = BOX * BOX // 128
MESH = pl.DeviceIdType.MESH
f32 = jnp.float32
bf16 = jnp.bfloat16


def cas_table(count):
    index = np.arange(count)
    angle = 2.0 * np.pi * ((index[:, None] * index[None, :]) % count) / count
    table = (np.cos(angle) + np.sin(angle)) / np.sqrt(count)
    high = table.astype(np.float32).astype(bf16)
    low = (table - high.astype(np.float64)).astype(np.float32).astype(bf16)
    return high, low


def split(values):
    high = values.astype(bf16)
    return high, (values - high.astype(f32)).astype(bf16)


def dot(a, b):
    return jnp.dot(a, b, preferred_element_type=f32)


def dot3(a, b):
    return dot(a[0], b[0]) + (dot(a[0], b[1]) + dot(a[1], b[0]))


def lanes(shape):
    return lax.broadcasted_iota(jnp.int32, shape, len(shape) - 1)


def rows(shape):
    return lax.broadcasted_iota(jnp.int32, shape, 0)


def wait_all(sem, ref):
    pltpu.make_async_copy(ref, ref, sem).wait()


def send(src, dst, send_sem, recv_sem, slab, sub):
    pltpu.make_async_remote_copy(
        src, dst, send_sem, recv_sem, device_id=(slab, sub), device_id_type=MESH
    ).start()


def far_first(j, count):
    return (count // 2 + (j + 1) // 2 * (1 - 2 * (j % 2))) % count


def partner(i, slab, sub, count):
    x, core, z, y = i % 4, i // 4 % 2, i // 8 % 8, i // 64
    zc = slab % 16
    target_z = (zc // 2 + far_first(z, 8)) % 8
    target_y = (slab // 16 + far_first(y, count // 64)) % (count // 64)
    target_core = (zc % 2 + 1 - core) % 2
    return (target_y * 8 + target_z) * 2 + target_core, (sub + far_first(x, 4)) % 4


def to_everyone(src, dst, slab, sub, count, send_sem, recv_sem):
    me = slab * SUBS + sub

    def one(i, carry):
        to_slab, to_sub = partner(i, slab, sub, count)
        send(
            src.at[pl.ds(to_slab * SUBS + to_sub, 1)],
            dst.at[pl.ds(me, 1)],
            send_sem,
            recv_sem,
            to_slab,
            to_sub,
        )
        return carry

    lax.fori_loop(0, count - 1, one, 0)
    dst[pl.ds(me, 1), :] = src[pl.ds(me, 1), :]
    wait_all(recv_sem, dst.at[pl.ds(0, count - 1)])


def wave_squares(index, count):
    folded = jnp.where(index > count // 2, index - count, index)
    wave = (2.0 * math.pi / (count * SPACING)) * folded.astype(f32)
    return wave * wave


def exchange_correlation(density):
    clipped = jnp.maximum(density, FLOOR)
    root = jnp.exp(jnp.log(clipped) * (1.0 / 3.0))
    radius = (3.0 / (4.0 * math.pi)) ** (1.0 / 3.0) / root
    exchange = -((3.0 / math.pi) ** (1.0 / 3.0)) * root
    inverse = 1.0 / (radius + 7.8)
    return exchange - 0.44 * inverse - (0.44 / 3.0) * radius * inverse * inverse


def density_rows(occupation_ref, sign_ref, orbital_ref, box):
    row = rows((ORB, 128))
    weight = jnp.zeros((ORB, 128), jnp.int32)
    for o in range(ORB):
        weight = jnp.where(row == o, occupation_ref[0, o] * sign_ref[0], weight)
    weight = weight.astype(f32)

    def one(g, carry):
        base = pl.multiple_of(g * 1024, 1024)
        values = orbital_ref[:, pl.ds(base, 1024)].astype(f32)
        out = pl.multiple_of(g * 8, 8)
        for j in range(8):
            part = values[:, j * 128 : j * 128 + 128]
            box[pl.ds(out + j, 1), :] = jnp.sum(weight * (part * part), axis=0, keepdims=True)
        return carry

    lax.fori_loop(FIRST * TILES // 8, BOX * TILES // 8, one, 0, unroll=2)


def core_planes(span_ref, corner_ref, box, staged, core, meta, slab, sub):
    own = slab * SUBS + sub
    first_z, first_x, first_y = span_ref[0, 0], span_ref[0, 1], span_ref[0, 2]
    long_z, long_x, long_y = span_ref[0, 3], span_ref[0, 4], span_ref[0, 5]
    offset = corner_ref[0, own] % Z_DEV
    planes = BOX - FIRST
    start = first_x * BOX + first_y
    tile, lane = start // 128, start % 128
    shape = (planes, 128)
    column = lanes(shape)
    turned = []
    for t in range(13):
        row = FIRST * TILES + jnp.minimum(tile + t, TILES - 1)
        raw = box[pl.ds(row, planes, stride=TILES), :]
        turned.append(pltpu.roll(raw, (128 - lane) % 128, 1))
    chunks = [jnp.where(column < 128 - lane, turned[t], turned[t + 1]) for t in range(12)]
    plane = rows(shape) + FIRST
    within_z = (plane >= first_z) & (plane < first_z + long_z)
    staged[pl.ds(0, 32), :] = jnp.zeros((32, 128), f32)
    staged[pl.ds(352, 32), :] = jnp.zeros((32, 128), f32)
    for t in range(8):
        value = jnp.zeros(shape, f32)
        for m in range(4):
            source = (4 * t + m) * BOX
            chunk, begin = source // 128, source % 128
            shift = (32 * m - begin) % 128
            piece = pltpu.roll(chunks[chunk], shift, 1)
            if begin + CORE > 128:
                after = pltpu.roll(chunks[chunk + 1], shift, 1)
                piece = jnp.where(column < 32 * m + 128 - begin, piece, after)
            value = jnp.where(column // 32 == m, piece, value)
        inside = within_z & (4 * t + column // 32 < long_x) & (column % 32 < long_y)
        staged[pl.ds(32 + t, planes, stride=8), :] = jnp.where(inside, value, 0.0)
    core[...] = staged[pl.ds((Z_DEV - offset) * 8, REACH * SUBS * 8), :]
    start_x = (corner_ref[1, own] + first_x) % NX
    start_y = (corner_ref[2, own] + first_y) % NY
    meta[...] = jnp.where(lanes((8, 128)) == 0, start_x, start_y)


def place_cores(first_cell, got, ring, wide):
    column = lanes((8, 128))
    ring[...] = jnp.zeros_like(ring)

    def place(d, carry):
        base = pl.multiple_of(d * 32, 32)
        cells = got[pl.ds(base, 8), :]
        for q in range(1, SUBS):
            cells = cells + got[pl.ds(base + 8 * q, 8), :]
        start_x, start_y = first_cell[d, 0], first_cell[d, 1]
        for m in range(4):
            piece = pltpu.roll(cells, (128 - 32 * m) % 128, 1)
            piece = jnp.where(column < 32, piece, 0.0)
            piece = jnp.concatenate([piece, jnp.zeros((8, 128), f32)], axis=1)
            piece = pltpu.roll(piece, start_y, 1)
            for half in range(2):
                side = piece[:, half * 128 : half * 128 + 128]
                ring[half, pl.ds(m, 8, stride=4), :] = side
                ring[half, pl.ds(NX + m, 8, stride=4), :] = side
        for half in range(2):
            wide[half, pl.ds(0, NX), :] = (
                wide[half, pl.ds(0, NX), :] + ring[half, pl.ds(NX - start_x, NX), :]
            )
        return carry

    lax.fori_loop(0, REACH, place, 0)


def whole_kernel(
    span_ref,
    corner_ref,
    occupation_ref,
    sign_ref,
    orbital_ref,
    outer_ref,
    high_ref,
    low_ref,
    high_z_ref,
    low_z_ref,
    box_out,
    grid_out,
    box,
    staged,
    core,
    meta,
    got,
    told,
    first_cell,
    outer,
    ring,
    wide,
    spec,
    got_z,
    turned,
    back,
    potential,
    cut,
    windows,
    frame,
    send_sem,
    recv_sem,
    local_sem,
):
    slab, sub = lax.axis_index("slab"), lax.axis_index("sub")
    slabs = lax.axis_size("slab")
    count = slabs * SUBS
    barrier = pltpu.get_barrier_semaphore()

    def greet(i, carry):
        pl.semaphore_signal(
            barrier, inc=1, device_id=partner(i, slab, sub, count), device_id_type=MESH
        )
        return carry

    lax.fori_loop(0, count - 1, greet, 0)
    density_rows(occupation_ref, sign_ref, orbital_ref, box)
    core_planes(span_ref, corner_ref, box, staged, core, meta, slab, sub)
    pl.semaphore_wait(barrier, count - 1)

    def pass_meta(j, carry):
        d = REACH - 1 - j
        to = (slab + NEAR + d) % slabs
        send(meta.at[pl.ds(0, 1)], told.at[pl.ds(d, 1)], send_sem.at[1], recv_sem.at[1], to, sub)
        return carry

    def pass_core(j, carry):
        p = REACH * SUBS - 1 - j
        src = core.at[pl.ds(p * 8, 8)]
        dst = got.at[pl.ds((p // SUBS * SUBS + sub) * 8, 8)]
        to = (slab + NEAR + p // SUBS) % slabs
        send(src, dst, send_sem.at[0], recv_sem.at[0], to, p % SUBS)
        return carry

    def pass_outer(k, carry):
        to = (sub + k) % SUBS
        dst = outer.at[pl.ds(sub * 64, 64)]
        send(outer_ref.at[to], dst, send_sem.at[2], recv_sem.at[2], slab, to)
        return carry

    lax.fori_loop(0, REACH, pass_meta, 0)
    lax.fori_loop(0, REACH * SUBS, pass_core, 0)
    lax.fori_loop(1, SUBS, pass_outer, 0)
    outer[pl.ds(pl.multiple_of(sub * 64, 64), 64), :] = outer_ref[sub]
    wait_all(recv_sem.at[2], outer.at[pl.ds(0, 192)])
    for half in range(2):
        wide[half, pl.ds(0, NX), :] = outer[:, pl.ds(half * 128, 128)]
    wait_all(recv_sem.at[1], told)
    tell = pltpu.make_async_copy(told, first_cell, local_sem)
    tell.start()
    tell.wait()
    wait_all(recv_sem.at[0], got)
    place_cores(first_cell, got, ring, wide)

    density = jnp.concatenate([wide[half, pl.ds(0, NX), :] for half in range(2)], axis=1)
    outer[...] = exchange_correlation(density)
    table = (high_ref[...], low_ref[...])
    values = dot3(table, split(dot3(split(density), table)))
    spec[pl.ds(0, NX), :] = values[:, :128]
    spec[pl.ds(NX, NX), :] = values[:, 128:]

    to_everyone(spec, got_z, slab, sub, count, send_sem.at[3], recv_sem.at[3])
    table_z = (high_z_ref[...], low_z_ref[...])
    values = dot3(table_z, split(got_z[...]))
    me = slab * SUBS + sub
    shape = (count, 128)
    square = (
        wave_squares(rows(shape), count)
        + wave_squares(jnp.zeros(shape, jnp.int32) + me % NX, NX)
        + wave_squares(lanes(shape) + me // NX * 128, NY)
    )
    factor = jnp.where(square > 0, 4.0 * math.pi / jnp.where(square > 0, square, 1.0), 0.0)
    turned[...] = dot3(table_z, split(values * factor))
    to_everyone(turned, back, slab, sub, count, send_sem.at[4], recv_sem.at[4])

    values = jnp.concatenate([back[pl.ds(0, NX), :], back[pl.ds(NX, NX), :]], axis=1)
    values = dot3(split(dot3(table, split(values))), table) + outer[...]
    potential[...] = values
    for half in range(2):
        side = values[:, half * 128 : half * 128 + 128]
        wide[half, pl.ds(0, NX), :] = side
        wide[half, pl.ds(NX, BOX), :] = side[:BOX]

    def pass_plane(k, carry):
        to = (sub + k) % SUBS
        src = potential.at[pl.ds(to * 64, 64)]
        send(src, grid_out.at[sub], send_sem.at[5], recv_sem.at[5], slab, to)
        return carry

    lax.fori_loop(1, SUBS, pass_plane, 0)

    column = lanes((24, 128))

    def windows_of(j, carry):
        d = jnp.where(j <= 8, 8 + (j + 1) // 2 * (1 - 2 * (j % 2)), SPREAD - 1 - j)
        to = (slab - d + slabs) % slabs
        for q in range(SUBS):
            fragment = to * SUBS + q
            start_x, start_y = corner_ref[1, fragment], corner_ref[2, fragment]
            here = pl.ds(start_x, BOX)
            strip = jnp.concatenate([wide[0, here, :], wide[1, here, :]], axis=1)
            strip = pltpu.roll(strip, (NY - start_y) % NY, 1)
            cut[pl.ds(q * BOX, BOX), :] = strip[:, :128]
        out = [jnp.zeros((24, 128), f32) for _ in range(3)]
        for b in range(8):
            tile, begin = b * BOX // 128, b * BOX % 128
            value = pltpu.roll(cut[pl.ds(b, 24, stride=8), :], begin, 1)
            here = (column >= begin) & (column < begin + BOX)
            out[tile] = jnp.where(here, value, out[tile])
            if begin + BOX > 128:
                out[tile + 1] = jnp.where(column < begin + BOX - 128, value, out[tile + 1])
        for t in range(3):
            windows[pl.ds(d * 72 + t, 24, stride=3), :] = out[t]

        def pass_window(q, carry):
            @pl.when((d > 0) | (q != sub))
            def _():
                src = windows.at[pl.ds((d * SUBS + q) * TILES, TILES)]
                dst = frame.at[pl.ds((d * SUBS + sub) * TILES, TILES)]
                send(src, dst, send_sem.at[6], recv_sem.at[6], to, q)

            return carry

        return lax.fori_loop(0, SUBS, pass_window, carry)

    lax.fori_loop(0, SPREAD, windows_of, 0)
    frame[pl.ds(sub * TILES, TILES), :] = windows[pl.ds(sub * TILES, TILES), :]
    grid_out[sub] = potential[pl.ds(pl.multiple_of(sub * 64, 64), 64), :]
    own_windows = frame.at[pl.ds(0, (SPREAD * SUBS - 1) * TILES)]
    wait_all(recv_sem.at[6], own_windows)
    offset = corner_ref[0, me] % Z_DEV
    box_out[...] = frame[pl.ds(offset * TILES, BOX * TILES), :]
    wait_all(recv_sem.at[5], grid_out.at[pl.ds(0, SUBS - 1)])
    wait_all(send_sem.at[0], got)
    wait_all(send_sem.at[1], told)
    wait_all(send_sem.at[2], outer.at[pl.ds(0, 192)])
    wait_all(send_sem.at[3], back.at[pl.ds(0, count - 1)])
    wait_all(send_sem.at[4], back.at[pl.ds(0, count - 1)])
    wait_all(send_sem.at[5], grid_out.at[pl.ds(0, SUBS - 1)])
    wait_all(send_sem.at[6], own_windows)


def body(orbitals, occupations, patch_sign, corners, core_span, outer_density):
    count = lax.axis_size("slab") * SUBS
    tables = [jnp.asarray(t) for t in (*cas_table(NX), *cas_table(count))]
    smem = pl.BlockSpec(memory_space=pltpu.SMEM)
    vmem = pl.BlockSpec(memory_space=pltpu.VMEM)
    cores = (REACH * SUBS * 8, 128)
    planes = (SPREAD * SUBS * TILES, 128)
    box_potential, potential = pl.pallas_call(
        whole_kernel,
        out_shape=[
            jax.ShapeDtypeStruct((BOX * TILES, 128), f32),
            jax.ShapeDtypeStruct((Z_DEV, NX // SUBS, NY), f32),
        ],
        in_specs=[smem] * 4 + [vmem] * 6,
        out_specs=[vmem] * 2,
        scratch_shapes=[
            pltpu.VMEM((BOX * TILES, 128), f32),
            pltpu.VMEM((384, 128), f32),
            pltpu.VMEM(cores, f32),
            pltpu.VMEM((8, 128), jnp.int32),
            pltpu.VMEM(cores, f32),
            pltpu.VMEM((REACH, 128), jnp.int32),
            pltpu.SMEM((REACH, 128), jnp.int32),
            pltpu.VMEM((NX, NY), f32),
            pltpu.VMEM((2, 2 * NX, 128), f32),
            pltpu.VMEM((2, NX + BOX, 128), f32),
            pltpu.VMEM((count, 128), f32),
            pltpu.VMEM((count, 128), f32),
            pltpu.VMEM((count, 128), f32),
            pltpu.VMEM((count, 128), f32),
            pltpu.VMEM((NX, NY), f32),
            pltpu.VMEM((SUBS * BOX, 128), f32),
            pltpu.VMEM(planes, f32),
            pltpu.VMEM(planes, f32),
            pltpu.SemaphoreType.DMA((7,)),
            pltpu.SemaphoreType.DMA((7,)),
            pltpu.SemaphoreType.DMA,
        ],
        compiler_params=pltpu.CompilerParams(collective_id=0, has_side_effects=True),
        name="whole",
    )(core_span, corners.T, occupations, patch_sign, orbitals[0], outer_density, *tables)
    return box_potential.reshape(1, BOX * BOX * BOX), potential


def solution(mesh):
    placed = (
        P(("slab", "sub"), None, None),
        P(("slab", "sub"), None),
        P(("slab", "sub")),
        P(),
        P(("slab", "sub"), None),
        P("slab", "sub", None),
    )
    return jax.shard_map(
        body,
        mesh=mesh,
        in_specs=placed,
        out_specs=(P(("slab", "sub"), None), P("slab", "sub", None)),
        check_vma=False,
    )
```

time: 504 us -> 177 us (0.35)
  the two profiles are of different devices: /device:TPU:24 before, /device:TPU:56 now
where the time goes in v2:
time: 177 us; the launch traced here: 176 us
  Pallas kernels  171 us (97%)
  local copies, waits for them, and re-layouts  3.48 us (2%)
    pallas_call x1, Pallas kernels, body(): pl.pallas_call(whole_kernel, out_shape=[jax.ShapeDtypeStruct((BOX * TILES...  171 us

profile of v2, /device:TPU:56, one launch (start us, length us, event | category | flops | bytes accessed | tf_op | source)
XLA Modules:
  0.0 176.1 jit_solution(1443392683243783626)
XLA Ops:
  1.3 171.3 %whole.1 = (f32[864,128]{1,0:T(8,128)}, f32[4,64,256]{2,1,0:T(8,128)}) custom-call(s32[1,6]{1,0:T(1,128)} %span_ref.1, s32[3,512]{1,0:T(4,128)} %bitcast.5, s32[1,16]{1,0:T(1,128)} %occupation_ref.1, s32[1]{0:T(128)S(6)} %copy.14.sign_ref, bf16[16,110592]{1,0:T(8,128)(2,1)} %bitcast.3, f32[4,64,256]{2,1,0:T(8,128)} %outer_ref.1, ...), custom_call_target="tpu_custom_call" | custom-call | tf_op jit(solution)/shard_map/whole/pallas_call | solution.py:384
  172.6 1.8 %copy.15 = f32[1,110592]{1,0:T(1,128)} copy(f32[1,110592]{1,0:T(1,128)} %bitcast.4) | data formatting | bytes 884736
  174.4 1.7 copy.16

commit v3 on v2

--- a/solution.py
+++ b/solution.py
@@ -67,37 +67,35 @@
     ).start()
 
 
-def far_first(j, count):
-    return (count // 2 + (j + 1) // 2 * (1 - 2 * (j % 2))) % count
-
-
-def partner(i, slab, sub, count):
-    x, core, z, y = i % 4, i // 4 % 2, i // 8 % 8, i // 64
-    zc = slab % 16
-    target_z = (zc // 2 + far_first(z, 8)) % 8
-    target_y = (slab // 16 + far_first(y, count // 64)) % (count // 64)
-    target_core = (zc % 2 + 1 - core) % 2
-    return (target_y * 8 + target_z) * 2 + target_core, (sub + far_first(x, 4)) % 4
-
-
-def to_everyone(src, dst, slab, sub, count, send_sem, recv_sem):
-    me = slab * SUBS + sub
-
-    def one(i, carry):
-        to_slab, to_sub = partner(i, slab, sub, count)
-        send(
-            src.at[pl.ds(to_slab * SUBS + to_sub, 1)],
-            dst.at[pl.ds(me, 1)],
-            send_sem,
-            recv_sem,
-            to_slab,
-            to_sub,
-        )
-        return carry
-
-    lax.fori_loop(0, count - 1, one, 0)
-    dst[pl.ds(me, 1), :] = src[pl.ds(me, 1), :]
-    wait_all(recv_sem, dst.at[pl.ds(0, count - 1)])
+def for_all_others(slab, sub, slabs, visit):
+    subs = [sub] + [lax.rem(sub + k, SUBS) for k in range(1, SUBS)]
+    line = 16
+    lines = slabs // line
+    here, row = lax.rem(slab, line), lax.div(slab, line)
+    steps = sorted(range(lines), key=lambda k: -min(k, lines - k))
+    for step in steps:
+        base = lax.rem(row + step, lines) * line
+
+        def one(i, carry):
+            target = base + lax.rem(here + i, line)
+            for k in (2, 1, 3, 0):
+                visit(target, subs[k])
+            return carry
+
+        lax.fori_loop(0 if step else 1, line, one, 0)
+    for k in range(1, SUBS):
+        visit(slab, subs[k])
+
+
+def to_everyone(src, dst, slab, sub, slabs, send_sem, recv_sem):
+    here = pl.ds(slab * SUBS + sub, 1)
+
+    def visit(to_slab, to_sub):
+        row = pl.ds(to_slab * SUBS + to_sub, 1)
+        send(src.at[row], dst.at[here], send_sem, recv_sem, to_slab, to_sub)
+
+    for_all_others(slab, sub, slabs, visit)
+    dst[here, :] = src[here, :]
 
 
 def wave_squares(index, count):
@@ -235,77 +233,89 @@
     send_sem,
     recv_sem,
     local_sem,
+    orbitals,
+    high,
+    low,
+    high_z,
+    low_z,
 ):
     slab, sub = lax.axis_index("slab"), lax.axis_index("sub")
     slabs = lax.axis_size("slab")
     count = slabs * SUBS
     barrier = pltpu.get_barrier_semaphore()
 
-    def greet(i, carry):
-        pl.semaphore_signal(
-            barrier, inc=1, device_id=partner(i, slab, sub, count), device_id_type=MESH
-        )
-        return carry
-
-    lax.fori_loop(0, count - 1, greet, 0)
-    density_rows(occupation_ref, sign_ref, orbital_ref, box)
+    loads = [
+        pltpu.make_async_copy(orbital_ref, orbitals, local_sem.at[0]),
+        pltpu.make_async_copy(high_ref, high, local_sem.at[1]),
+        pltpu.make_async_copy(low_ref, low, local_sem.at[2]),
+        pltpu.make_async_copy(high_z_ref, high_z, local_sem.at[3]),
+        pltpu.make_async_copy(low_z_ref, low_z, local_sem.at[4]),
+        pltpu.make_async_copy(outer_ref.at[sub], outer.at[pl.ds(sub * 64, 64)], local_sem.at[5]),
+    ]
+    for load in loads:
+        load.start()
+
+    def greet(to_slab, to_sub):
+        pl.semaphore_signal(barrier, inc=1, device_id=(to_slab, to_sub), device_id_type=MESH)
+
+    for_all_others(slab, sub, slabs, greet)
+    loads[0].wait()
+    density_rows(occupation_ref, sign_ref, orbitals, box)
     core_planes(span_ref, corner_ref, box, staged, core, meta, slab, sub)
     pl.semaphore_wait(barrier, count - 1)
 
-    def pass_meta(j, carry):
+    def pass_cores(j, carry):
         d = REACH - 1 - j
-        to = (slab + NEAR + d) % slabs
+        to = lax.rem(slab + NEAR + d, slabs)
         send(meta.at[pl.ds(0, 1)], told.at[pl.ds(d, 1)], send_sem.at[1], recv_sem.at[1], to, sub)
-        return carry
-
-    def pass_core(j, carry):
-        p = REACH * SUBS - 1 - j
-        src = core.at[pl.ds(p * 8, 8)]
-        dst = got.at[pl.ds((p // SUBS * SUBS + sub) * 8, 8)]
-        to = (slab + NEAR + p // SUBS) % slabs
-        send(src, dst, send_sem.at[0], recv_sem.at[0], to, p % SUBS)
+        for q in range(SUBS):
+            src = core.at[pl.ds((d * SUBS + q) * 8, 8)]
+            dst = got.at[pl.ds((d * SUBS + sub) * 8, 8)]
+            send(src, dst, send_sem.at[0], recv_sem.at[0], to, q)
         return carry
 
     def pass_outer(k, carry):
-        to = (sub + k) % SUBS
+        to = lax.rem(sub + k, SUBS)
         dst = outer.at[pl.ds(sub * 64, 64)]
         send(outer_ref.at[to], dst, send_sem.at[2], recv_sem.at[2], slab, to)
         return carry
 
-    lax.fori_loop(0, REACH, pass_meta, 0)
-    lax.fori_loop(0, REACH * SUBS, pass_core, 0)
+    lax.fori_loop(0, REACH, pass_cores, 0)
     lax.fori_loop(1, SUBS, pass_outer, 0)
-    outer[pl.ds(pl.multiple_of(sub * 64, 64), 64), :] = outer_ref[sub]
+    for load in loads[1:]:
+        load.wait()
     wait_all(recv_sem.at[2], outer.at[pl.ds(0, 192)])
     for half in range(2):
         wide[half, pl.ds(0, NX), :] = outer[:, pl.ds(half * 128, 128)]
     wait_all(recv_sem.at[1], told)
-    tell = pltpu.make_async_copy(told, first_cell, local_sem)
+    tell = pltpu.make_async_copy(told, first_cell, local_sem.at[6])
     tell.start()
     tell.wait()
     wait_all(recv_sem.at[0], got)
     place_cores(first_cell, got, ring, wide)
 
     density = jnp.concatenate([wide[half, pl.ds(0, NX), :] for half in range(2)], axis=1)
-    outer[...] = exchange_correlation(density)
-    table = (high_ref[...], low_ref[...])
+    table = (high[...], low[...])
     values = dot3(table, split(dot3(split(density), table)))
     spec[pl.ds(0, NX), :] = values[:, :128]
     spec[pl.ds(NX, NX), :] = values[:, 128:]
 
-    to_everyone(spec, got_z, slab, sub, count, send_sem.at[3], recv_sem.at[3])
-    table_z = (high_z_ref[...], low_z_ref[...])
-    values = dot3(table_z, split(got_z[...]))
+    to_everyone(spec, got_z, slab, sub, slabs, send_sem.at[3], recv_sem.at[3])
+    outer[...] = exchange_correlation(density)
     me = slab * SUBS + sub
     shape = (count, 128)
     square = (
         wave_squares(rows(shape), count)
-        + wave_squares(jnp.zeros(shape, jnp.int32) + me % NX, NX)
-        + wave_squares(lanes(shape) + me // NX * 128, NY)
+        + wave_squares(jnp.zeros(shape, jnp.int32) + lax.rem(me, NX), NX)
+        + wave_squares(lanes(shape) + lax.div(me, NX) * 128, NY)
     )
-    factor = jnp.where(square > 0, 4.0 * math.pi / jnp.where(square > 0, square, 1.0), 0.0)
-    turned[...] = dot3(table_z, split(values * factor))
-    to_everyone(turned, back, slab, sub, count, send_sem.at[4], recv_sem.at[4])
+    turned[...] = jnp.where(square > 0, 4.0 * math.pi / jnp.where(square > 0, square, 1.0), 0.0)
+    wait_all(recv_sem.at[3], got_z.at[pl.ds(0, count - 1)])
+    table_z = (high_z[...], low_z[...])
+    values = dot3(table_z, split(got_z[...])) * turned[...]
+    turned[...] = dot3(table_z, split(values))
+    to_everyone(turned, back, slab, sub, slabs, send_sem.at[4], recv_sem.at[4])
+    wait_all(recv_sem.at[4], back.at[pl.ds(0, count - 1)])
 
     values = jnp.concatenate([back[pl.ds(0, NX), :], back[pl.ds(NX, NX), :]], axis=1)
     values = dot3(split(dot3(table, split(values))), table) + outer[...]
@@ -316,7 +326,7 @@
         wide[half, pl.ds(NX, BOX), :] = side[:BOX]
 
     def pass_plane(k, carry):
-        to = (sub + k) % SUBS
+        to = lax.rem(sub + k, SUBS)
         src = potential.at[pl.ds(to * 64, 64)]
         send(src, grid_out.at[sub], send_sem.at[5], recv_sem.at[5], slab, to)
         return carry
@@ -326,8 +336,9 @@
     column = lanes((24, 128))
 
     def windows_of(j, carry):
-        d = jnp.where(j <= 8, 8 + (j + 1) // 2 * (1 - 2 * (j % 2)), SPREAD - 1 - j)
-        to = (slab - d + slabs) % slabs
+        swing = lax.div(j + 1, 2) * (1 - 2 * lax.rem(j, 2))
+        d = jnp.where(j <= 8, 8 + swing, SPREAD - 1 - j)
+        to = lax.rem(slab - d + slabs, slabs)
         for q in range(SUBS):
             fragment = to * SUBS + q
             start_x, start_y = corner_ref[1, fragment], corner_ref[2, fragment]
@@ -346,16 +357,15 @@
         for t in range(3):
             windows[pl.ds(d * 72 + t, 24, stride=3), :] = out[t]
 
-        def pass_window(q, carry):
-            @pl.when((d > 0) | (q != sub))
+        for q in range(SUBS):
+            src = windows.at[pl.ds((d * SUBS + q) * TILES, TILES)]
+            dst = frame.at[pl.ds((d * SUBS + sub) * TILES, TILES)]
+
+            @pl.when((d > 0) | (sub != q))
             def _():
-                src = windows.at[pl.ds((d * SUBS + q) * TILES, TILES)]
-                dst = frame.at[pl.ds((d * SUBS + sub) * TILES, TILES)]
                 send(src, dst, send_sem.at[6], recv_sem.at[6], to, q)
 
-            return carry
-
-        return lax.fori_loop(0, SUBS, pass_window, carry)
+        return carry
 
     lax.fori_loop(0, SPREAD, windows_of, 0)
     frame[pl.ds(sub * TILES, TILES), :] = windows[pl.ds(sub * TILES, TILES), :]
@@ -387,7 +397,7 @@
             jax.ShapeDtypeStruct((BOX * TILES, 128), f32),
             jax.ShapeDtypeStruct((Z_DEV, NX // SUBS, NY), f32),
         ],
-        in_specs=[smem] * 4 + [vmem] * 6,
+        in_specs=[smem] * 4 + [pl.BlockSpec(memory_space=pl.ANY)] * 6,
         out_specs=[vmem] * 2,
         scratch_shapes=[
             pltpu.VMEM((BOX * TILES, 128), f32),
@@ -410,7 +420,12 @@
             pltpu.VMEM(planes, f32),
             pltpu.SemaphoreType.DMA((7,)),
             pltpu.SemaphoreType.DMA((7,)),
-            pltpu.SemaphoreType.DMA,
+            pltpu.SemaphoreType.DMA((7,)),
+            pltpu.VMEM((ORB, BOX * BOX * BOX), bf16),
+            pltpu.VMEM((NX, NY), bf16),
+            pltpu.VMEM((NX, NY), bf16),
+            pltpu.VMEM((count, count), bf16),
+            pltpu.VMEM((count, count), bf16),
         ],
         compiler_params=pltpu.CompilerParams(collective_id=0, has_side_effects=True),
         name="whole",

time: 177 us -> 85.5 us (0.48)
  Pallas kernels: 171 us -> 79.4 us
    pallas_call x1, Pallas kernels: 171 us -> 79.4 us  [body(): pl.pallas_call(whole_kernel, out_shape=[jax.ShapeDtypeStruct((BOX * TILES...]
where the time goes in v3:
time: 85.5 us; the launch traced here: 84.2 us
  Pallas kernels  79.4 us (93%)
  local copies, waits for them, and re-layouts  3.48 us (4%)
  between operations  1.28 us (1%)
    pallas_call x1, Pallas kernels, body(): pl.pallas_call(whole_kernel, out_shape=[jax.ShapeDtypeStruct((BOX * TILES...  79.4 us
    unnamed x2, local copies, waits for them, and re-layouts  3.48 us

profile of v3, /device:TPU:56, one launch (start us, length us, event | category | flops | bytes accessed | tf_op | source)
XLA Modules:
  0.0 84.2 jit_solution(6410172982783209526)
XLA Ops:
  1.3 79.4 %whole.1 = (f32[864,128]{1,0:T(8,128)}, f32[4,64,256]{2,1,0:T(8,128)}) custom-call(s32[1,6]{1,0:T(1,128)} %span_ref.1, s32[3,512]{1,0:T(4,128)} %bitcast.5, s32[1,16]{1,0:T(1,128)} %occupation_ref.1, s32[1]{0:T(128)S(6)} %copy.14.sign_ref, bf16[16,110592]{1,0:T(8,128)(2,1)} %bitcast.3, f32[4,64,256]{2,1,0:T(8,128)} %outer_ref.1, ...), custom_call_target="tpu_custom_call" | custom-call | tf_op jit(solution)/shard_map/whole/pallas_call | solution.py:394
  80.7 1.8 %copy.15 = f32[1,110592]{1,0:T(1,128)} copy(f32[1,110592]{1,0:T(1,128)} %bitcast.4) | data formatting | bytes 884736
  82.5 1.7 %copy.16 = f32[4,64,256]{2,1,0:T(8,128)} copy(f32[4,64,256]{2,1,0:T(8,128)} %get-tuple-element.9) | data formatting | bytes 524288

commit v4 on v3

--- a/solution.py
+++ b/solution.py
@@ -14,6 +14,7 @@
 NY = 256
 Z_DEV = 4
 SUBS = 4
+LINE = 16
 CORE = 32
 FIRST = 8
 SPACING = 0.35
@@ -69,20 +70,19 @@
 
 def for_all_others(slab, sub, slabs, visit):
     subs = [sub] + [lax.rem(sub + k, SUBS) for k in range(1, SUBS)]
-    line = 16
-    lines = slabs // line
-    here, row = lax.rem(slab, line), lax.div(slab, line)
+    lines = slabs // LINE
+    here, row = lax.rem(slab, LINE), lax.div(slab, LINE)
     steps = sorted(range(lines), key=lambda k: -min(k, lines - k))
     for step in steps:
-        base = lax.rem(row + step, lines) * line
+        base = lax.rem(row + step, lines) * LINE
 
         def one(i, carry):
-            target = base + lax.rem(here + i, line)
+            target = base + lax.rem(here + i, LINE)
             for k in (2, 1, 3, 0):
                 visit(target, subs[k])
             return carry
 
-        lax.fori_loop(0 if step else 1, line, one, 0)
+        lax.fori_loop(0 if step else 1, LINE, one, 0)
     for k in range(1, SUBS):
         visit(slab, subs[k])
 
@@ -117,7 +117,7 @@
     row = rows((ORB, 128))
     weight = jnp.zeros((ORB, 128), jnp.int32)
     for o in range(ORB):
-        weight = jnp.where(row == o, occupation_ref[0, o] * sign_ref[0], weight)
+        weight = jnp.where(row == o, occupation_ref[0, o] * sign_ref[0, 0], weight)
     weight = weight.astype(f32)
 
     def one(g, carry):
@@ -210,7 +210,7 @@
     low_ref,
     high_z_ref,
     low_z_ref,
-    box_out,
+    frame,
     grid_out,
     box,
     staged,
@@ -229,10 +229,10 @@
     potential,
     cut,
     windows,
-    frame,
     send_sem,
     recv_sem,
     local_sem,
+    column_sem,
     orbitals,
     high,
     low,
@@ -255,14 +255,31 @@
     for load in loads:
         load.start()
 
-    def greet(to_slab, to_sub):
-        pl.semaphore_signal(barrier, inc=1, device_id=(to_slab, to_sub), device_id_type=MESH)
-
-    for_all_others(slab, sub, slabs, greet)
+    def greet(sem, to_slab, to_sub):
+        pl.semaphore_signal(sem, inc=1, device_id=(to_slab, to_sub), device_id_type=MESH)
+
+    lines = slabs // LINE
+    here, row = lax.rem(slab, LINE), lax.div(slab, LINE)
+    column = [lax.rem(row + k, lines) * LINE + here for k in range(1, lines)]
+
+    def greet_row(i, carry):
+        target = row * LINE + lax.rem(here + i, LINE)
+        for k in range(SUBS):
+            greet(barrier, target, lax.rem(sub + k, SUBS))
+        return carry
+
+    for target in column:
+        greet(barrier, target, sub)
+    lax.fori_loop(1, LINE, greet_row, 0)
+    for k in range(1, SUBS):
+        greet(barrier, slab, lax.rem(sub + k, SUBS))
     loads[0].wait()
     density_rows(occupation_ref, sign_ref, orbitals, box)
+    pl.semaphore_wait(barrier, LINE * SUBS - 1 + lines - 1)
+    for target in column:
+        greet(column_sem, target, sub)
     core_planes(span_ref, corner_ref, box, staged, core, meta, slab, sub)
-    pl.semaphore_wait(barrier, count - 1)
+    pl.semaphore_wait(column_sem, lines - 1)
 
     def pass_cores(j, carry):
         d = REACH - 1 - j
@@ -368,12 +385,17 @@
         return carry
 
     lax.fori_loop(0, SPREAD, windows_of, 0)
-    frame[pl.ds(sub * TILES, TILES), :] = windows[pl.ds(sub * TILES, TILES), :]
-    grid_out[sub] = potential[pl.ds(pl.multiple_of(sub * 64, 64), 64), :]
+    own = pl.ds(sub * TILES, TILES)
+    keeps = [
+        pltpu.make_async_copy(windows.at[own], frame.at[own], local_sem.at[0]),
+        pltpu.make_async_copy(
+            potential.at[pl.ds(sub * 64, 64)], grid_out.at[sub], local_sem.at[1]
+        ),
+    ]
+    for keep in keeps:
+        keep.start()
     own_windows = frame.at[pl.ds(0, (SPREAD * SUBS - 1) * TILES)]
     wait_all(recv_sem.at[6], own_windows)
-    offset = corner_ref[0, me] % Z_DEV
-    box_out[...] = frame[pl.ds(offset * TILES, BOX * TILES), :]
     wait_all(recv_sem.at[5], grid_out.at[pl.ds(0, SUBS - 1)])
     wait_all(send_sem.at[0], got)
     wait_all(send_sem.at[1], told)
@@ -382,23 +404,44 @@
     wait_all(send_sem.at[4], back.at[pl.ds(0, count - 1)])
     wait_all(send_sem.at[5], grid_out.at[pl.ds(0, SUBS - 1)])
     wait_all(send_sem.at[6], own_windows)
+    for keep in keeps:
+        keep.wait()
+
+
+def finish_kernel(corner_ref, frame_ref, grid_ref, box_out, grid_out, box, grid, into, out):
+    me = lax.axis_index("slab") * SUBS + lax.axis_index("sub")
+    offset = corner_ref[0, me] % Z_DEV
+    half = BOX * TILES // 2
+    moves = [(frame_ref.at[pl.ds(offset * TILES + k * half, half)], box.at[pl.ds(k * half, half)]) for k in range(2)]
+    moves.append((grid_ref, grid))
+    ends = [box_out.at[pl.ds(0, half)], box_out.at[pl.ds(half, half)], grid_out]
+    reads = [pltpu.make_async_copy(a, b, into.at[k]) for k, (a, b) in enumerate(moves)]
+    writes = [pltpu.make_async_copy(moves[k][1], ends[k], out.at[k]) for k in range(3)]
+    for read in reads:
+        read.start()
+    for read, write in zip(reads, writes):
+        read.wait()
+        write.start()
+    for write in writes:
+        write.wait()
 
 
 def body(orbitals, occupations, patch_sign, corners, core_span, outer_density):
     count = lax.axis_size("slab") * SUBS
     tables = [jnp.asarray(t) for t in (*cas_table(NX), *cas_table(count))]
     smem = pl.BlockSpec(memory_space=pltpu.SMEM)
-    vmem = pl.BlockSpec(memory_space=pltpu.VMEM)
+    hbm = pl.BlockSpec(memory_space=pl.ANY)
     cores = (REACH * SUBS * 8, 128)
     planes = (SPREAD * SUBS * TILES, 128)
-    box_potential, potential = pl.pallas_call(
+    grid_shape = jax.ShapeDtypeStruct((Z_DEV, NX // SUBS, NY), f32)
+    frame, potential = pl.pallas_call(
         whole_kernel,
         out_shape=[
-            jax.ShapeDtypeStruct((BOX * TILES, 128), f32),
-            jax.ShapeDtypeStruct((Z_DEV, NX // SUBS, NY), f32),
+            jax.ShapeDtypeStruct(planes, f32),
+            grid_shape,
         ],
-        in_specs=[smem] * 4 + [pl.BlockSpec(memory_space=pl.ANY)] * 6,
-        out_specs=[vmem] * 2,
+        in_specs=[smem] * 4 + [hbm] * 6,
+        out_specs=[hbm] * 2,
         scratch_shapes=[
             pltpu.VMEM((BOX * TILES, 128), f32),
             pltpu.VMEM((384, 128), f32),
@@ -417,10 +460,10 @@
             pltpu.VMEM((NX, NY), f32),
             pltpu.VMEM((SUBS * BOX, 128), f32),
             pltpu.VMEM(planes, f32),
-            pltpu.VMEM(planes, f32),
             pltpu.SemaphoreType.DMA((7,)),
             pltpu.SemaphoreType.DMA((7,)),
             pltpu.SemaphoreType.DMA((7,)),
+            pltpu.SemaphoreType.REGULAR,
             pltpu.VMEM((ORB, BOX * BOX * BOX), bf16),
             pltpu.VMEM((NX, NY), bf16),
             pltpu.VMEM((NX, NY), bf16),
@@ -429,7 +472,20 @@
         ],
         compiler_params=pltpu.CompilerParams(collective_id=0, has_side_effects=True),
         name="whole",
-    )(core_span, corners.T, occupations, patch_sign, orbitals[0], outer_density, *tables)
+    )(core_span, corners.T, occupations, patch_sign.reshape(1, 1), orbitals[0], outer_density, *tables)
+    box_potential, potential = pl.pallas_call(
+        finish_kernel,
+        out_shape=[jax.ShapeDtypeStruct((BOX * TILES, 128), f32), grid_shape],
+        in_specs=[smem, hbm, hbm],
+        out_specs=[hbm, hbm],
+        scratch_shapes=[
+            pltpu.VMEM((BOX * TILES, 128), f32),
+            pltpu.VMEM(grid_shape.shape, f32),
+            pltpu.SemaphoreType.DMA((3,)),
+            pltpu.SemaphoreType.DMA((3,)),
+        ],
+        name="finish",
+    )(corners.T, frame, potential)
     return box_potential.reshape(1, BOX * BOX * BOX), potential
 
 

time: 85.5 us -> 82.2 us (0.961)
  local copies, waits for them, and re-layouts: 3.48 us -> 0 us
  Pallas kernels: 79.4 us -> 80.3 us
    unnamed x2 -> x0, local copies, waits for them, and re-layouts: 3.48 us -> none
    pallas_call x1 -> x2, Pallas kernels: 79.4 us -> 80.3 us  [the longest x1 77.6 us: body(): pl.pallas_call(whole_kernel, out_shape=[jax.ShapeDtypeStruct(planes, f32)...]
where the time goes in v4:
time: 82.2 us; the launch traced here: 81.6 us
  Pallas kernels  80.3 us (98%)
  between operations  1.28 us (2%)
    pallas_call x1, Pallas kernels, body(): pl.pallas_call(whole_kernel, out_shape=[jax.ShapeDtypeStruct(planes, f32)...  77.6 us
    pallas_call x1, Pallas kernels, body(): pl.pallas_call(finish_kernel, out_shape=[jax.ShapeDtypeStruct((BOX * TILE...  2.74 us

profile of v4, /device:TPU:56, one launch (start us, length us, event | category | flops | bytes accessed | tf_op | source)
XLA Modules:
  0.0 81.6 jit_solution(473501744967867048)
XLA Ops:
  1.3 77.6 %whole.1 = (f32[936,128]{1,0:T(8,128)}, f32[4,64,256]{2,1,0:T(8,128)}) custom-call(s32[1,6]{1,0:T(1,128)} %span_ref.1, s32[3,512]{1,0:T(4,128)} %bitcast.6, s32[1,16]{1,0:T(1,128)} %occupation_ref.1, s32[1,1]{1,0:T(1,128)} %bitcast.4.sign_ref, bf16[16,110592]{1,0:T(8,128)(2,1)} %bitcast.5, f32[4,64,256]{2,1,0:T(8,128)} %outer_ref.1, ...), custom_call_target="tpu_custom_call" | custom-call | tf_op jit(solution)/shard_map/whole/pallas_call | solution.py:437
  78.9 2.7 %finish.1 = (f32[864,128]{1,0:T(8,128)}, f32[4,64,256]{2,1,0:T(8,128)}) custom-call(s32[3,512]{1,0:T(4,128)} %bitcast.7, f32[936,128]{1,0:T(8,128)} %get-tuple-element.6.frame_ref, f32[4,64,256]{2,1,0:T(8,128)} %get-tuple-element.7.grid_ref), custom_call_target="tpu_custom_call" | custom-call | tf_op jit(solution)/shard_map/finish/pallas_call | solution.py:476

commit v5 on v4

--- a/solution.py
+++ b/solution.py
@@ -68,23 +68,31 @@
     ).start()
 
 
+def far_first(j, count):
+    return count // 2 + lax.div(j + 1, 2) * (1 - 2 * lax.rem(j, 2))
+
+
 def for_all_others(slab, sub, slabs, visit):
     subs = [sub] + [lax.rem(sub + k, SUBS) for k in range(1, SUBS)]
-    lines = slabs // LINE
-    here, row = lax.rem(slab, LINE), lax.div(slab, LINE)
-    steps = sorted(range(lines), key=lambda k: -min(k, lines - k))
-    for step in steps:
-        base = lax.rem(row + step, lines) * LINE
-
-        def one(i, carry):
-            target = base + lax.rem(here + i, LINE)
+    lines, chips = slabs // LINE, LINE // 2
+    row, chip, core = lax.div(slab, LINE), lax.div(lax.rem(slab, LINE), 2), lax.rem(slab, 2)
+
+    for level in range(lines + chips - 2):
+
+        def one(j, carry):
+            to_row = lax.rem(row + far_first(j, lines), lines)
+            to_chip = lax.rem(chip + far_first(level - j, chips), chips)
+            base = (to_row * chips + to_chip) * 2
             for k in (2, 1, 3, 0):
-                visit(target, subs[k])
+                for c in range(2):
+                    visit(base + c, subs[k])
             return carry
 
-        lax.fori_loop(0 if step else 1, LINE, one, 0)
-    for k in range(1, SUBS):
+        lax.fori_loop(max(level - (chips - 1), 0), min(level, lines - 1) + 1, one, 0)
+    for k in (2, 1, 3):
         visit(slab, subs[k])
+    for k in (2, 1, 3, 0):
+        visit(slab + 1 - 2 * core, subs[k])
 
 
 def to_everyone(src, dst, slab, sub, slabs, send_sem, recv_sem):
@@ -171,9 +179,8 @@
     meta[...] = jnp.where(lanes((8, 128)) == 0, start_x, start_y)
 
 
-def place_cores(first_cell, got, ring, wide):
+def place_cores(first_cell, got, ring, wide, spans):
     column = lanes((8, 128))
-    ring[...] = jnp.zeros_like(ring)
 
     def place(d, carry):
         base = pl.multiple_of(d * 32, 32)
@@ -196,7 +203,8 @@
             )
         return carry
 
-    lax.fori_loop(0, REACH, place, 0)
+    for span in spans:
+        lax.fori_loop(*span, place, 0)
 
 
 def whole_kernel(
@@ -281,15 +289,21 @@
     core_planes(span_ref, corner_ref, box, staged, core, meta, slab, sub)
     pl.semaphore_wait(column_sem, lines - 1)
 
-    def pass_cores(j, carry):
-        d = REACH - 1 - j
-        to = lax.rem(slab + NEAR + d, slabs)
-        send(meta.at[pl.ds(0, 1)], told.at[pl.ds(d, 1)], send_sem.at[1], recv_sem.at[1], to, sub)
-        for q in range(SUBS):
-            src = core.at[pl.ds((d * SUBS + q) * 8, 8)]
-            dst = got.at[pl.ds((d * SUBS + sub) * 8, 8)]
-            send(src, dst, send_sem.at[0], recv_sem.at[0], to, q)
-        return carry
+    batches = (((4, 9),), ((0, 4), (9, REACH)))
+
+    def pass_cores(batch):
+        def one(d, carry):
+            to = lax.rem(slab + NEAR + d, slabs)
+            recv = recv_sem.at[7 + 2 * batch]
+            send(meta.at[pl.ds(0, 1)], told.at[pl.ds(d, 1)], send_sem.at[1], recv, to, sub)
+            for q in range(SUBS):
+                src = core.at[pl.ds((d * SUBS + q) * 8, 8)]
+                dst = got.at[pl.ds((d * SUBS + sub) * 8, 8)]
+                send(src, dst, send_sem.at[0], recv_sem.at[8 + 2 * batch], to, q)
+            return carry
+
+        for span in batches[batch]:
+            lax.fori_loop(*span, one, 0)
 
     def pass_outer(k, carry):
         to = lax.rem(sub + k, SUBS)
@@ -297,19 +311,29 @@
         send(outer_ref.at[to], dst, send_sem.at[2], recv_sem.at[2], slab, to)
         return carry
 
-    lax.fori_loop(0, REACH, pass_cores, 0)
+    pass_cores(0)
+    pass_cores(1)
     lax.fori_loop(1, SUBS, pass_outer, 0)
+    ring[...] = jnp.zeros_like(ring)
     for load in loads[1:]:
         load.wait()
     wait_all(recv_sem.at[2], outer.at[pl.ds(0, 192)])
     for half in range(2):
         wide[half, pl.ds(0, NX), :] = outer[:, pl.ds(half * 128, 128)]
-    wait_all(recv_sem.at[1], told)
-    tell = pltpu.make_async_copy(told, first_cell, local_sem.at[6])
-    tell.start()
-    tell.wait()
-    wait_all(recv_sem.at[0], got)
-    place_cores(first_cell, got, ring, wide)
+    for batch in (1, 0):
+        spans = batches[batch]
+        size = sum(end - start for start, end in spans)
+        wait_all(recv_sem.at[7 + 2 * batch], told.at[pl.ds(0, size)])
+        tells = []
+        for k, (start, end) in enumerate(spans):
+            part = pl.ds(start, end - start)
+            sem = local_sem.at[6 + batch + k]
+            tells.append(pltpu.make_async_copy(told.at[part], first_cell.at[part], sem))
+            tells[-1].start()
+        for tell in tells:
+            tell.wait()
+        wait_all(recv_sem.at[8 + 2 * batch], got.at[pl.ds(0, size * SUBS * 8)])
+        place_cores(first_cell, got, ring, wide, spans)
 
     density = jnp.concatenate([wide[half, pl.ds(0, NX), :] for half in range(2)], axis=1)
     table = (high[...], low[...])
@@ -461,8 +485,8 @@
             pltpu.VMEM((SUBS * BOX, 128), f32),
             pltpu.VMEM(planes, f32),
             pltpu.SemaphoreType.DMA((7,)),
-            pltpu.SemaphoreType.DMA((7,)),
-            pltpu.SemaphoreType.DMA((7,)),
+            pltpu.SemaphoreType.DMA((11,)),
+            pltpu.SemaphoreType.DMA((9,)),
             pltpu.SemaphoreType.REGULAR,
             pltpu.VMEM((ORB, BOX * BOX * BOX), bf16),
             pltpu.VMEM((NX, NY), bf16),

time: 82.2 us -> 81.8 us (level)
  no operation moved by 1% of the time
where the time goes in v5:
time: 81.8 us; the launch traced here: 81.5 us
  Pallas kernels  80.3 us (98%)
  between operations  1.28 us (2%)
    pallas_call x1, Pallas kernels, body(): pl.pallas_call(whole_kernel, out_shape=[jax.ShapeDtypeStruct(planes, f32)...  77.5 us
    pallas_call x1, Pallas kernels, body(): pl.pallas_call(finish_kernel, out_shape=[jax.ShapeDtypeStruct((BOX * TILE...  2.74 us

profile of v5, /device:TPU:56, one launch (start us, length us, event | category | flops | bytes accessed | tf_op | source)
XLA Modules:
  0.0 81.5 jit_solution(6905347739421567394)
XLA Ops:
  1.3 77.5 %whole.1 = (f32[936,128]{1,0:T(8,128)}, f32[4,64,256]{2,1,0:T(8,128)}) custom-call(s32[1,6]{1,0:T(1,128)} %span_ref.1, s32[3,512]{1,0:T(4,128)} %bitcast.6, s32[1,16]{1,0:T(1,128)} %occupation_ref.1, s32[1,1]{1,0:T(1,128)} %bitcast.4.sign_ref, bf16[16,110592]{1,0:T(8,128)(2,1)} %bitcast.5, f32[4,64,256]{2,1,0:T(8,128)} %outer_ref.1, ...), custom_call_target="tpu_custom_call" | custom-call | tf_op jit(solution)/shard_map/whole/pallas_call | solution.py:461
  78.8 2.7 %finish.1 = (f32[864,128]{1,0:T(8,128)}, f32[4,64,256]{2,1,0:T(8,128)}) custom-call(s32[3,512]{1,0:T(4,128)} %bitcast.7, f32[936,128]{1,0:T(8,128)} %get-tuple-element.6.frame_ref, f32[4,64,256]{2,1,0:T(8,128)} %get-tuple-element.7.grid_ref), custom_call_target="tpu_custom_call" | custom-call | tf_op jit(solution)/shard_map/finish/pallas_call | solution.py:500

commit v6 on v5

--- a/solution.py
+++ b/solution.py
@@ -377,8 +377,7 @@
     column = lanes((24, 128))
 
     def windows_of(j, carry):
-        swing = lax.div(j + 1, 2) * (1 - 2 * lax.rem(j, 2))
-        d = jnp.where(j <= 8, 8 + swing, SPREAD - 1 - j)
+        d = SPREAD - 1 - j
         to = lax.rem(slab - d + slabs, slabs)
         for q in range(SUBS):
             fragment = to * SUBS + q

time: 81.8 us -> 79.9 us (0.977)
  the two profiles are of different devices: /device:TPU:56 before, /device:TPU:1 now
where the time goes in v6:
time: 79.9 us; the launch traced here: 79.5 us
  Pallas kernels  78.2 us (98%)
  between operations  1.28 us (2%)
    pallas_call x1, Pallas kernels, body(): pl.pallas_call(whole_kernel, out_shape=[jax.ShapeDtypeStruct(planes, f32)...  75.5 us
    pallas_call x1, Pallas kernels, body(): pl.pallas_call(finish_kernel, out_shape=[jax.ShapeDtypeStruct((BOX * TILE...  2.74 us

profile of v6, /device:TPU:1, one launch (start us, length us, event | category | flops | bytes accessed | tf_op | source)
XLA Modules:
  0.0 79.5 jit_solution(6573104395414552368)
XLA Ops:
  1.3 75.5 %whole.1 = (f32[936,128]{1,0:T(8,128)}, f32[4,64,256]{2,1,0:T(8,128)}) custom-call(s32[1,6]{1,0:T(1,128)} %span_ref.1, s32[3,512]{1,0:T(4,128)} %bitcast.6, s32[1,16]{1,0:T(1,128)} %occupation_ref.1, s32[1,1]{1,0:T(1,128)} %bitcast.4.sign_ref, bf16[16,110592]{1,0:T(8,128)(2,1)} %bitcast.5, f32[4,64,256]{2,1,0:T(8,128)} %outer_ref.1, ...), custom_call_target="tpu_custom_call" | custom-call | tf_op jit(solution)/shard_map/whole/pallas_call | solution.py:460
  76.8 2.7 %finish.1 = (f32[864,128]{1,0:T(8,128)}, f32[4,64,256]{2,1,0:T(8,128)}) custom-call(s32[3,512]{1,0:T(4,128)} %bitcast.7, f32[936,128]{1,0:T(8,128)} %get-tuple-element.6.frame_ref, f32[4,64,256]{2,1,0:T(8,128)} %get-tuple-element.7.grid_ref), custom_call_target="tpu_custom_call" | custom-call | tf_op jit(solution)/shard_map/finish/pallas_call | solution.py:499
